TPU v7x, 256 devices: a whole 4x4x8 slice. The times are simulated.
256 devices in a mesh: il: 2 (over core), xl: 4 (over x), ta: 32 (over z, y).
Axes of the slice: x: 4, y: 4, z: 8, core: 2. Of those that a mesh axis runs over, the one named last changes fastest.
Arguments:
- traces: float32 [32, 832, 8192], P('il', 'xl', 'ta'), may hold values from -6 to 6
- bin_steps: int32 [2, 32, 832], P(None, 'il', 'xl'), may hold values from -1 to 1
Outputs:
- regridded: float32 [16, 416, 12288], P('il', 'xl', 'ta')
Inputs may be any that keep to these rules, and one draw needn't show every extreme that they name: `bin_steps`: every entry is -1, 0 or 1.
All inputs are finite; a program needn't handle non-finite values.
Results may differ from a plain program's by a relative error of at most 0.0001.
Values sent between devices are 32-bit elements; how exact they have to be, the bound alone decides.
A program may use at most 128 MiB of HBM per device.

v0:
```python
import jax
import jax.numpy as jnp
from jax import lax
from jax.sharding import PartitionSpec as P

TAPS = 16
P_SIZE = 3
Q = 2


def extended(shard, sides, width):
    for axis, dim in sides:
        devices, length = (lax.axis_size(axis), shard.shape[dim])
        up = [(i, (i + 1) % devices) for i in range(devices - 1)]
        down = [(j, i) for i, j in up]
        last = lax.slice_in_dim(shard, length - width, length, axis=dim)
        first = lax.slice_in_dim(shard, 0, width, axis=dim)
        before = lax.ppermute(last, axis, up)
        after = lax.ppermute(first, axis, down)
        shard = jnp.concatenate([before, shard, after], axis=dim)
    return shard


def shifted(shard, axis, by):
    devices = lax.axis_size(axis)
    pairs = [(i, i + by) for i in range(devices) if 0 <= i + by < devices]
    return lax.ppermute(shard, axis, pairs)


def lanczos_table(row_count, col_count, tap_reach, ratio_p, ratio_q):
    row_ids = lax.broadcasted_iota(jnp.int32, (row_count, col_count), 0)
    col_ids = lax.broadcasted_iota(jnp.int32, (row_count, col_count), 1)
    offset = (col_ids * ratio_q - (row_ids - tap_reach) * ratio_p).astype(
        jnp.float32
    ) / jnp.float32(ratio_p)
    inside = jnp.abs(offset) < jnp.float32(tap_reach)
    weights = jnp.sinc(offset) * jnp.sinc(offset / jnp.float32(tap_reach))
    return jnp.where(inside, weights, jnp.zeros_like(weights))


def widen_time(values, tap_reach):
    return extended(values, (("ta", 2),), tap_reach)


def resample(widened, tap_reach):
    row_count, col_count, length = widened.shape
    span = length - 2 * tap_reach
    block = 128
    count = span // block
    out_len = block * P_SIZE // Q
    taps_table = lanczos_table(block + 2 * tap_reach, out_len, tap_reach, P_SIZE, Q)
    flat_rows = widened.reshape(row_count * col_count, length)
    windows = jnp.stack(
        [flat_rows[:, k * block : k * block + block + 2 * tap_reach] for k in range(count)], axis=1
    )
    result = jnp.dot(
        windows, taps_table, precision=lax.Precision.HIGHEST, preferred_element_type=jnp.float32
    )
    return result.reshape(row_count, col_count, count * out_len)


def bin_sums(values, bin_steps):
    row_count, col_count, length = values.shape
    half_rows = row_count // 2
    half_cols = col_count // 2
    bin_total = jnp.zeros((half_rows + 2, half_cols + 2, length), jnp.float32)
    fold_count = jnp.zeros((half_rows + 2, half_cols + 2), jnp.float32)
    for row_phase in (0, 1):
        for col_phase in (0, 1):
            sub_values = values[row_phase::2, col_phase::2]
            step_il = bin_steps[0, row_phase::2, col_phase::2]
            step_xl = bin_steps[1, row_phase::2, col_phase::2]
            for shift_il in (-1, 0, 1):
                for shift_xl in (-1, 0, 1):
                    chosen = ((step_il == shift_il) & (step_xl == shift_xl)).astype(jnp.float32)
                    widths = ((1 + shift_il, 1 - shift_il), (1 + shift_xl, 1 - shift_xl))
                    bin_total = bin_total + jnp.pad(
                        sub_values * chosen[:, :, None], widths + ((0, 0),)
                    )
                    fold_count = fold_count + jnp.pad(chosen, widths)
    return (bin_total, fold_count)


def fold_rims(bin_total, fold_count):
    from_lower = shifted((bin_total[:, -1:], fold_count[:, -1:]), "xl", 1)
    from_upper = shifted((bin_total[:, :1], fold_count[:, :1]), "xl", -1)
    owned_sums = bin_total[:, 1:-1].at[:, :1].add(from_lower[0]).at[:, -1:].add(from_upper[0])
    owned_folds = fold_count[:, 1:-1].at[:, :1].add(from_lower[1]).at[:, -1:].add(from_upper[1])
    from_lower = shifted((owned_sums[-1:], owned_folds[-1:]), "il", 1)
    from_upper = shifted((owned_sums[:1], owned_folds[:1]), "il", -1)
    owned_sums = owned_sums[1:-1].at[:1].add(from_lower[0]).at[-1:].add(from_upper[0])
    owned_folds = owned_folds[1:-1].at[:1].add(from_lower[1]).at[-1:].add(from_upper[1])
    return (owned_sums, owned_folds)


def shards(traces, bin_steps):
    tap_reach = TAPS // 2
    bin_total, fold_count = bin_sums(traces, bin_steps)
    owned_sums, owned_folds = fold_rims(bin_total, fold_count)
    stacked = owned_sums / jnp.maximum(owned_folds, 1.0)[:, :, None]
    return resample(widen_time(stacked, tap_reach), tap_reach)


def solution(mesh):
    return jax.shard_map(
        shards,
        mesh=mesh,
        in_specs=(P("il", "xl", "ta"), P(None, "il", "xl")),
        out_specs=P("il", "xl", "ta"),
        check_vma=False,
    )
```

profile of v0, /device:TPU:126, one launch (start us, length us, event | category | flops | bytes accessed | tf_op | source)
XLA Modules:
  0.0 96.6 jit_solution(2746602787613257369)
XLA Ops:
  0.0 0.9 slice.261
  0.9 0.9 slice.262
  1.8 0.9 slice.264
  2.7 0.9 slice.265
  3.6 0.9 slice.267
  4.5 0.9 slice.268
  5.4 0.9 slice.270
  6.3 0.9 slice.271
  7.3 0.0 copy-start.4
  7.4 0.0 copy-start.5
  7.4 0.5 copy-done.4
  7.9 0.1 pad_add_fusion.1
  8.1 0.7 fusion.77
  8.7 1.4 %collective-permute-start.4 = (f32[10,1]{1,0:T(8,128)}, f32[10,1]{1,0:T(8,128)}, u32[]{:S(2)}, u32[]{:S(2)}) collective-permute-start(f32[10,1]{1,0:T(8,128)} %get-tuple-element.193), channel_id=1, source_target_pairs={{0,32},{32,64},{64,96},{1,33},{33,65},{65,97},{2,34},{34,66},{66,9... | collective-permute-start | bytes 128 | tf_op jit(solution)/shard_map/ppermute | solution.py:27
  10.2 5.1 %collective-permute-start.5 = (f32[10,1]{1,0:T(8,128)}, f32[10,1]{1,0:T(8,128)}, u32[]{:S(2)}, u32[]{:S(2)}) collective-permute-start(f32[10,1]{1,0:T(8,128)} %get-tuple-element.192), channel_id=1, source_target_pairs={{32,0},{64,32},{96,64},{33,1},{65,33},{97,65},{34,2},{66,34},{98,6... | collective-permute-start | bytes 128 | tf_op jit(solution)/shard_map/ppermute | solution.py:27
  15.3 5.6 %slice.260 = f32[8,104,256]{2,1,0:T(8,128)} slice(f32[16,208,256]{2,1,0:T(8,128)} %param.19), slice={[0:16:2], [0:208:2], [0:256:1]} | slice | bytes 1703936 | tf_op jit(solution)/shard_map/slice | solution.py:70
  20.9 5.6 %slice.263 = f32[8,104,256]{2,1,0:T(8,128)} slice(f32[16,208,256]{2,1,0:T(8,128)} %param.19), slice={[0:16:2], [1:208:2], [0:256:1]} | slice | bytes 1703936 | tf_op jit(solution)/shard_map/slice | solution.py:70
  26.5 0.0 copy-done
  26.5 3.3 %slice.266 = f32[8,104,256]{2,1,0:T(8,128)} slice(f32[16,208,256]{2,1,0:T(8,128)S(1)} %copy-done), slice={[1:16:2], [0:208:2], [0:256:1]} | slice | bytes 1703936 | tf_op jit(solution)/shard_map/slice | solution.py:70
  29.8 3.3 %slice.269 = f32[8,104,256]{2,1,0:T(8,128)} slice(f32[16,208,256]{2,1,0:T(8,128)S(1)} %copy-done), slice={[1:16:2], [1:208:2], [0:256:1]} | slice | bytes 1703936 | tf_op jit(solution)/shard_map/slice | solution.py:70
  33.1 2.3 %broadcast_multiply_fusion.35 = (f32[8,104,256]{2,1,0:T(8,128)S(1)}, f32[8,104,256]{2,1,0:T(8,128)S(1)}, f32[8,104,256]{2,1,0:T(8,128)S(1)}, f32[8,104,256]{2,1,...) fusion(f32[8,104,256]{2,1,0:T(8,128)} %slice.260, ...), kind=kLoop, calls=%fused_computation.42 | loop fusion | flops 1916928 | bytes 8549632 | tf_op jit(solution)/shard_map/mul | solution.py:78
  35.4 0.0 copy-done.3
  35.4 0.0 copy-start.2
  35.4 1.2 %broadcast_multiply_fusion.26 = (f32[8,104,256]{2,1,0:T(8,128)S(1)}, f32[8,104,256]{2,1,0:T(8,128)S(1)}, f32[8,104,256]{2,1,0:T(8,128)S(1)}, f32[8,104,256]{2,1,...) fusion(f32[8,104,256]{2,1,0:T(8,128)S(1)} %copy-done.3, ...), kind=kLoop, calls=%fused_computation.33 | loop fusion | flops 1916928 | bytes 8549632 | tf_op jit(solution)/shard_map/mul | solution.py:78
  36.6 0.0 copy-start.1
  36.7 2.8 %broadcast_multiply_fusion.17 = (f32[8,104,256]{2,1,0:T(8,128)S(1)}, f32[8,104,256]{2,1,0:T(8,128)S(1)}, f32[8,104,256]{2,1,0:T(8,128)S(1)}, f32[8,104,256]{2,1,...) fusion(f32[8,104,256]{2,1,0:T(8,128)S(1)} %copy-done.2, ...), kind=kLoop, calls=%fused_computation.24 | loop fusion | flops 1916928 | bytes 8549632 | tf_op jit(solution)/shard_map/mul | solution.py:78
  39.5 3.6 %broadcast_multiply_fusion.8 = (f32[8,104,256]{2,1,0:T(8,128)}, f32[8,104,256]{2,1,0:T(8,128)}, f32[8,104,256]{2,1,0:T(8,128)}, f32[8,104,256]{2,1,0:T(8,128)}, ...) fusion(f32[8,104,256]{2,1,0:T(8,128)S(1)} %copy-done.1, ...), kind=kLoop, calls=%fused_computation.15 | loop fusion | flops 1916928 | bytes 8549632 | tf_op jit(solution)/shard_map/mul | solution.py:78
  43.1 7.2 %pad_add_fusion = f32[10,106,256]{2,1,0:T(8,128)S(1)} fusion(f32[8,104,256]{2,1,0:T(8,128)} %get-tuple-element.182, f32[8,104,256]{2,1,0:T(8,128)} %get-tuple-element.183, f32[8,104,256]{2,1,0:T(8,128)} %get-tuple-element.184, f32[8,104,256]{2,1,0:T(8,128)} %get-tuple-element.185, f32[8,104,256]{2,1,0:T(8,128)} %get-tuple-element.186, ...), kind=kLoop, calls=%fused_computation.1 | loop fusion | flops 9497600 | bytes 31756288 | tf_op jit(solution)/shard_map/add | solution.py:77
  50.3 1.3 %collective-permute-start = (f32[10,1,256]{2,1,0:T(1,128)S(1)}, f32[10,1,256]{2,1,0:T(1,128)S(1)}, u32[]{:S(2)}, u32[]{:S(2)}) collective-permute-start(f32[10,1,256]{2,1,0:T(1,128)S(1)} %get-tuple-element.149), channel_id=1, source_target_pairs={{0,32},{32,64},{64,96},{1,33},{33,65},{65,97},{2,34},{34,66},{66,9... | collective-permute-start | bytes 30728 | tf_op jit(solution)/shard_map/ppermute | solution.py:27
  51.6 4.5 %collective-permute-start.1 = (f32[10,1,256]{2,1,0:T(1,128)S(1)}, f32[10,1,256]{2,1,0:T(1,128)S(1)}, u32[]{:S(2)}, u32[]{:S(2)}) collective-permute-start(f32[10,1,256]{2,1,0:T(1,128)S(1)} %get-tuple-element.148), channel_id=1, source_target_pairs={{32,0},{64,32},{96,64},{33,1},{65,33},{97,65},{34,2},{66,34},{98,6... | collective-permute-start | bytes 30728 | tf_op jit(solution)/shard_map/ppermute | solution.py:27
  56.2 0.6 compare_reduce_fusion
  56.8 0.1 slice.306
  56.9 0.0 collective-permute-done.4
  56.9 1.4 %add_select_fusion = f32[10,1]{1,0:T(8,128)S(1)} fusion(f32[10,1]{1,0:T(8,128)} %collective-permute-done.4, f32[10,106]{1,0:T(8,128)S(1)} %pad_add_fusion.1, pred[]{:T(512)} %compare_reduce_fusion), kind=kLoop, calls=%fused_computation.117 | loop fusion | flops 20 | bytes 121 | tf_op jit(solution)/shard_map/select.12
  58.4 0.0 collective-permute-done.5
  58.4 0.8 slice_add_fusion.4
  59.1 0.1 scatter-add.35
  59.2 1.3 %collective-permute-start.6 = (f32[1,104]{1,0:T(1,128)S(1)}, f32[1,104]{1,0:T(1,128)S(1)}, u32[]{:S(2)}, u32[]{:S(2)}) collective-permute-start(f32[1,104]{1,0:T(1,128)S(1)} %get-tuple-element.191), channel_id=1, source_target_pairs={{0,128},{1,129},{2,130},{3,131},{4,132},{5,133},{6,134},{7,135},{8... | collective-permute-start | bytes 1256 | tf_op jit(solution)/shard_map/ppermute | solution.py:27
  60.5 0.1 slice.296
  60.6 1.3 %collective-permute-start.7 = (f32[1,104]{1,0:T(1,128)S(1)}, f32[1,104]{1,0:T(1,128)S(1)}, u32[]{:S(2)}, u32[]{:S(2)}) collective-permute-start(f32[1,104]{1,0:T(1,128)S(1)} %get-tuple-element.190), channel_id=1, source_target_pairs={{128,0},{129,1},{130,2},{131,3},{132,4},{133,5},{134,6},{135,7},{1... | collective-permute-start | bytes 1256 | tf_op jit(solution)/shard_map/ppermute | solution.py:27
  61.9 0.0 collective-permute-done.6
  62.0 1.7 %collective-permute-done.7 = f32[1,104]{1,0:T(1,128)S(1)} collective-permute-done((f32[1,104]{1,0:T(1,128)S(1)}, f32[1,104]{1,0:T(1,128)S(1)}, u32[]{:S(2)}, u32[]{:S(2)}) %collective-permute-start.7) | collective-permute-done | bytes 448 | tf_op jit(solution)/shard_map/ppermute | solution.py:27
  63.7 0.0 collective-permute-done
  63.8 0.1 scatter-add.26
  63.8 0.0 collective-permute-done.1
  63.9 0.1 scatter-add.29
  64.0 2.1 %collective-permute-start.2 = (f32[1,104,256]{2,1,0:T(8,128)S(1)}, f32[1,104,256]{2,1,0:T(8,128)S(1)}, u32[]{:S(2)}, u32[]{:S(2)}) collective-permute-start(f32[1,104,256]{2,1,0:T(8,128)S(1)} %get-tuple-element.151), channel_id=1, source_target_pairs={{0,128},{1,129},{2,130},{3,131},{4,132},{5,133},{6,134},{7,135},{8... | collective-permute-start | bytes 319496 | tf_op jit(solution)/shard_map/ppermute | solution.py:27
  66.1 0.1 slice.301
  66.1 1.3 %collective-permute-start.3 = (f32[1,104,256]{2,1,0:T(8,128)S(1)}, f32[1,104,256]{2,1,0:T(8,128)S(1)}, u32[]{:S(2)}, u32[]{:S(2)}) collective-permute-start(f32[1,104,256]{2,1,0:T(8,128)S(1)} %get-tuple-element.150), channel_id=1, source_target_pairs={{128,0},{129,1},{130,2},{131,3},{132,4},{133,5},{134,6},{135,7},{1... | collective-permute-start | bytes 319496 | tf_op jit(solution)/shard_map/ppermute | solution.py:27
  67.4 0.0 collective-permute-done.2
  67.5 1.9 %collective-permute-done.3 = f32[1,104,256]{2,1,0:T(8,128)S(1)} collective-permute-done((f32[1,104,256]{2,1,0:T(8,128)S(1)}, f32[1,104,256]{2,1,0:T(8,128)S(1)}, u32[]{:S(2)}, u32[]{:S(2)}) %collective-permute-start.3) | collective-permute-done | bytes 106528 | tf_op jit(solution)/shard_map/ppermute | solution.py:27
  69.4 0.2 broadcast_divide_fusion
  69.5 0.2 fusion.75
  69.7 4.7 %collective-permute-start.8 = (f32[8,104,8]{2,1,0:T(8,128)S(1)}, f32[8,104,8]{2,1,0:T(8,128)S(1)}, u32[]{:S(2)}, u32[]{:S(2)}) collective-permute-start(f32[8,104,8]{2,1,0:T(8,128)S(1)} %get-tuple-element.152), channel_id=1, source_target_pairs={{0,1},{1,2},{2,3},{3,4},{4,5},{5,6},{6,7},{7,8},{8,9},{9,10},{10,1... | collective-permute-start | bytes 79880 | tf_op jit(solution)/shard_map/ppermute | solution.py:18
  74.4 1.9 %collective-permute-start.9 = (f32[8,104,8]{2,1,0:T(8,128)S(1)}, f32[8,104,8]{2,1,0:T(8,128)S(1)}, u32[]{:S(2)}, u32[]{:S(2)}) collective-permute-start(f32[8,104,8]{2,1,0:T(8,128)S(1)} %get-tuple-element.153), channel_id=1, source_target_pairs={{1,0},{2,1},{3,2},{4,3},{5,4},{6,5},{7,6},{8,7},{9,8},{10,9},{11,1... | collective-permute-start | bytes 79880 | tf_op jit(solution)/shard_map/ppermute | solution.py:19
  76.4 7.4 %collective-permute-done.8 = f32[8,104,8]{2,1,0:T(8,128)S(1)} collective-permute-done((f32[8,104,8]{2,1,0:T(8,128)S(1)}, f32[8,104,8]{2,1,0:T(8,128)S(1)}, u32[]{:S(2)}, u32[]{:S(2)}) %collective-permute-start.8) | collective-permute-done | bytes 26656 | tf_op jit(solution)/shard_map/ppermute | solution.py:18
  83.8 7.4 %collective-permute-done.9 = f32[8,104,8]{2,1,0:T(8,128)S(1)} collective-permute-done((f32[8,104,8]{2,1,0:T(8,128)S(1)}, f32[8,104,8]{2,1,0:T(8,128)S(1)}, u32[]{:S(2)}, u32[]{:S(2)}) %collective-permute-start.9) | collective-permute-done | bytes 26656 | tf_op jit(solution)/shard_map/ppermute | solution.py:19
  91.2 0.5 pad_maximum_fusion
  91.7 0.1 fusion.72
  91.9 0.3 copy.8
  92.1 0.3 copy.9
  92.4 1.8 %fusion = f32[832,2,192]{0,2,1:T(8,128)S(1)} fusion(f32[832,1,144]{0,2,1:T(8,128)S(1)} %bitcast.82, f32[832,1,144]{0,2,1:T(8,128)S(1)} %bitcast.81, s32[144]{0:T(256)S(1)} %add_multiply_fusion, s32[192]{0:T(256)S(1)} %iota_multiply_fusion), kind=kOutput, calls=%fused_computation.2 | convolution fusion | flops 554333184 | bytes 2237760 | tf_op jit(solution)/shard_map/dot_general | solution.py:56
  94.2 0.8 reshape.710
  95.0 1.6 %copy.6 = f32[8,104,384]{2,1,0:T(8,128)} copy(f32[8,104,384]{1,0,2:T(8,128)S(1)} %reshape.710) | data formatting | bytes 2555904 | tf_op jit(solution)/shard_map/reshape | solution.py:59
  (33 shorter events, 0.4 us)
Async XLA Ops:
  7.3 0.6 copy-start.4
  7.4 0.7 copy-start.5
  7.9 18.6 %copy-start = (f32[16,208,256]{2,1,0:T(8,128)S(1)}, f32[16,208,256]{2,1,0:T(8,128)}, u32[]{:S(2)}) copy-start(f32[16,208,256]{2,1,0:T(8,128)} %param.19) | copy-start | bytes 10223620
  8.7 48.1 %collective-permute-start.4 = (f32[10,1]{1,0:T(8,128)}, f32[10,1]{1,0:T(8,128)}, u32[]{:S(2)}, u32[]{:S(2)}) collective-permute-start(f32[10,1]{1,0:T(8,128)} %get-tuple-element.193), channel_id=1, source_target_pairs={{0,32},{32,64},{64,96},{1,33},{33,65},{65,97},{2,34},{34,66},{66,9... | collective-permute-start | bytes 128 | tf_op jit(solution)/shard_map/ppermute | solution.py:27
  10.2 48.2 %collective-permute-start.5 = (f32[10,1]{1,0:T(8,128)}, f32[10,1]{1,0:T(8,128)}, u32[]{:S(2)}, u32[]{:S(2)}) collective-permute-start(f32[10,1]{1,0:T(8,128)} %get-tuple-element.192), channel_id=1, source_target_pairs={{32,0},{64,32},{96,64},{33,1},{65,33},{97,65},{34,2},{66,34},{98,6... | collective-permute-start | bytes 128 | tf_op jit(solution)/shard_map/ppermute | solution.py:27
  33.1 2.3 %copy-start.3 = (f32[8,104,256]{2,1,0:T(8,128)S(1)}, f32[8,104,256]{2,1,0:T(8,128)}, u32[]{:S(2)}) copy-start(f32[8,104,256]{2,1,0:T(8,128)} %slice.263) | copy-start | bytes 2555908
  35.4 1.2 %copy-start.2 = (f32[8,104,256]{2,1,0:T(8,128)S(1)}, f32[8,104,256]{2,1,0:T(8,128)}, u32[]{:S(2)}) copy-start(f32[8,104,256]{2,1,0:T(8,128)} %slice.266) | copy-start | bytes 2555908
  36.6 2.8 %copy-start.1 = (f32[8,104,256]{2,1,0:T(8,128)S(1)}, f32[8,104,256]{2,1,0:T(8,128)}, u32[]{:S(2)}) copy-start(f32[8,104,256]{2,1,0:T(8,128)} %slice.269) | copy-start | bytes 2555908
  50.3 13.4 %collective-permute-start = (f32[10,1,256]{2,1,0:T(1,128)S(1)}, f32[10,1,256]{2,1,0:T(1,128)S(1)}, u32[]{:S(2)}, u32[]{:S(2)}) collective-permute-start(f32[10,1,256]{2,1,0:T(1,128)S(1)} %get-tuple-element.149), channel_id=1, source_target_pairs={{0,32},{32,64},{64,96},{1,33},{33,65},{65,97},{2,34},{34,66},{66,9... | collective-permute-start | bytes 30728 | tf_op jit(solution)/shard_map/ppermute | solution.py:27
  51.6 12.2 %collective-permute-start.1 = (f32[10,1,256]{2,1,0:T(1,128)S(1)}, f32[10,1,256]{2,1,0:T(1,128)S(1)}, u32[]{:S(2)}, u32[]{:S(2)}) collective-permute-start(f32[10,1,256]{2,1,0:T(1,128)S(1)} %get-tuple-element.148), channel_id=1, source_target_pairs={{32,0},{64,32},{96,64},{33,1},{65,33},{97,65},{34,2},{66,34},{98,6... | collective-permute-start | bytes 30728 | tf_op jit(solution)/shard_map/ppermute | solution.py:27
  59.2 2.7 %collective-permute-start.6 = (f32[1,104]{1,0:T(1,128)S(1)}, f32[1,104]{1,0:T(1,128)S(1)}, u32[]{:S(2)}, u32[]{:S(2)}) collective-permute-start(f32[1,104]{1,0:T(1,128)S(1)} %get-tuple-element.191), channel_id=1, source_target_pairs={{0,128},{1,129},{2,130},{3,131},{4,132},{5,133},{6,134},{7,135},{8... | collective-permute-start | bytes 1256 | tf_op jit(solution)/shard_map/ppermute | solution.py:27
  60.6 3.1 %collective-permute-start.7 = (f32[1,104]{1,0:T(1,128)S(1)}, f32[1,104]{1,0:T(1,128)S(1)}, u32[]{:S(2)}, u32[]{:S(2)}) collective-permute-start(f32[1,104]{1,0:T(1,128)S(1)} %get-tuple-element.190), channel_id=1, source_target_pairs={{128,0},{129,1},{130,2},{131,3},{132,4},{133,5},{134,6},{135,7},{1... | collective-permute-start | bytes 1256 | tf_op jit(solution)/shard_map/ppermute | solution.py:27
  64.0 3.5 %collective-permute-start.2 = (f32[1,104,256]{2,1,0:T(8,128)S(1)}, f32[1,104,256]{2,1,0:T(8,128)S(1)}, u32[]{:S(2)}, u32[]{:S(2)}) collective-permute-start(f32[1,104,256]{2,1,0:T(8,128)S(1)} %get-tuple-element.151), channel_id=1, source_target_pairs={{0,128},{1,129},{2,130},{3,131},{4,132},{5,133},{6,134},{7,135},{8... | collective-permute-start | bytes 319496 | tf_op jit(solution)/shard_map/ppermute | solution.py:27
  66.1 3.2 %collective-permute-start.3 = (f32[1,104,256]{2,1,0:T(8,128)S(1)}, f32[1,104,256]{2,1,0:T(8,128)S(1)}, u32[]{:S(2)}, u32[]{:S(2)}) collective-permute-start(f32[1,104,256]{2,1,0:T(8,128)S(1)} %get-tuple-element.150), channel_id=1, source_target_pairs={{128,0},{129,1},{130,2},{131,3},{132,4},{133,5},{134,6},{135,7},{1... | collective-permute-start | bytes 319496 | tf_op jit(solution)/shard_map/ppermute | solution.py:27
  69.7 14.1 %collective-permute-start.8 = (f32[8,104,8]{2,1,0:T(8,128)S(1)}, f32[8,104,8]{2,1,0:T(8,128)S(1)}, u32[]{:S(2)}, u32[]{:S(2)}) collective-permute-start(f32[8,104,8]{2,1,0:T(8,128)S(1)} %get-tuple-element.152), channel_id=1, source_target_pairs={{0,1},{1,2},{2,3},{3,4},{4,5},{5,6},{6,7},{7,8},{8,9},{9,10},{10,1... | collective-permute-start | bytes 79880 | tf_op jit(solution)/shard_map/ppermute | solution.py:18
  74.4 16.8 %collective-permute-start.9 = (f32[8,104,8]{2,1,0:T(8,128)S(1)}, f32[8,104,8]{2,1,0:T(8,128)S(1)}, u32[]{:S(2)}, u32[]{:S(2)}) collective-permute-start(f32[8,104,8]{2,1,0:T(8,128)S(1)} %get-tuple-element.153), channel_id=1, source_target_pairs={{1,0},{2,1},{3,2},{4,3},{5,4},{6,5},{7,6},{8,7},{9,8},{10,9},{11,1... | collective-permute-start | bytes 79880 | tf_op jit(solution)/shard_map/ppermute | solution.py:19
where the time goes:
time: 97.7 us; the launch traced here: 96.6 us
  local copies, waits for them, and re-layouts  30 us (31%)
  starting transfers between devices  25 us (26%)
  other arithmetic  20.9 us (21%)
  waiting for transfers between devices  18.5 us (19%)
  matrix products  1.78 us (2%)
    ppermute x8, starting transfers between devices, shifted(): return lax.ppermute(shard, axis, pairs)  18.4 us
    slice x4, local copies, waits for them, and re-layouts, bin_sums(): sub_values = values[row_phase::2, col_phase::2]  17.8 us
    mul x4, other arithmetic, bin_sums(): sub_values * chosen[:, :, None]  9.91 us
    ppermute x1, waiting for transfers between devices, extended(): after = lax.ppermute(first, axis, down)  7.44 us
    ppermute x1, waiting for transfers between devices, extended(): before = lax.ppermute(last, axis, up)  7.43 us
    add x1, other arithmetic, bin_sums(): bin_total + jnp.pad(sub_values * chosen[:, :, None], widths + ((0, 0),))  7.18 us
    ppermute x1, starting transfers between devices, extended(): before = lax.ppermute(last, axis, up)  4.69 us
    slice x4, local copies, waits for them, and re-layouts, bin_sums(): step_xl = bin_steps[1, row_phase::2, col_phase::2]  3.59 us
  transfers between devices with their start and end apart: 10, of which 4 were waited for; matrix products, arithmetic and copies ran while one was open for 40% of the time, Pallas kernels for 0%

commit v1 on v0

v1 whole, which is shorter than its diff:
```python
import functools

import jax
import jax.numpy as jnp
import numpy as np
from jax import lax
from jax.experimental import pallas as pl
from jax.experimental.pallas import tpu as pltpu
from jax.sharding import PartitionSpec as P

TAPS = 16
P_SIZE = 3
Q = 2
REACH = TAPS // 2

LANES = 128
ROWS, COLS, SPAN = 16, 208, 256
BROWS, BCOLS, OUT = 8, 104, 384
HALF = 64
SPLIT = 56
LOW_RIM, HIGH_RIM = 56, 112
FIRST_BIN, LAST_BIN = 0, 111
WINDOWS = ((0, 120), (104, 208))
GROUPS = tuple(range(0, 56, 8)) + tuple(range(64, 112, 8))

OFFSETS = tuple(
    (di, dx, dt) for di in (0, 1) for dx in (-1, 0, 1) for dt in (-1, 0, 1) if (di, dx, dt) != (0, 0, 0)
)


def filter_table():
    lane = np.arange(LANES)
    sample = np.stack(
        [
            np.where(lane < 112, lane, lane - 128),
            np.where(lane < 64, lane + 128, lane),
            np.where(lane < 16, lane + 256, lane + 128),
        ]
    )
    output = np.arange(OUT).reshape(3, LANES)
    x = (Q * output[:, None, :] - P_SIZE * sample[:, :, None]) / P_SIZE
    weights = np.where(np.abs(x) < REACH, np.sinc(x) * np.sinc(x / REACH), 0.0).astype(np.float32)
    high = weights.astype(jnp.bfloat16)
    low = (weights - high.astype(np.float32)).astype(jnp.bfloat16)
    top = np.concatenate([high, low], axis=2)
    bottom = np.concatenate([high, np.zeros_like(low)], axis=2)
    return np.concatenate([top, bottom], axis=1)


def parts_of(values):
    high = values.astype(jnp.bfloat16)
    low = (values - high.astype(jnp.float32)).astype(jnp.bfloat16)
    return high, low


def both(*conditions):
    held = [c for c in conditions if c is not None]
    return functools.reduce(jnp.logical_and, held) if held else None


def guarded(condition, action):
    if condition is None:
        action()
    else:
        pl.when(condition)(action)


def kernel(
    n_xl, n_ta, traces, steps, table, out,
    x, sv, cbuf, tab, onehot, acc, rims, corner, packed, packed_rim,
    ra, rb, rc, rd, re, rf, rg, load_sem, send_sem, recv_sem,
):
    il, xl, ta = lax.axis_index("il"), lax.axis_index("xl"), lax.axis_index("ta")

    steps_copy = pltpu.make_async_copy(steps, sv, load_sem.at[0])
    steps_copy.start()
    loads = []
    for k in range(BROWS):
        rows = pl.ds(2 * k, 2)
        loads.append(pltpu.make_async_copy(traces.at[rows], x.at[rows], load_sem.at[k + 1]))
        loads[-1].start()
    table_copy = pltpu.make_async_copy(table, tab, load_sem.at[BROWS + 1])
    table_copy.start()

    def there(step, index, size):
        return None if step == 0 else (index > 0 if step < 0 else index < size - 1)

    def sends_to(offset):
        return both(there(offset[1], xl, n_xl), there(offset[2], ta, n_ta))

    def hears_from(offset):
        return both(there(-offset[1], xl, n_xl), there(-offset[2], ta, n_ta))

    def device(offset):
        return {"il": 1 - il if offset[0] else il, "xl": xl + offset[1], "ta": ta + offset[2]}

    barrier = pltpu.get_barrier_semaphore()
    for offset in OFFSETS:
        guarded(
            sends_to(offset),
            functools.partial(
                pl.semaphore_signal, barrier, 1, device_id=device(offset), device_id_type=pl.DeviceIdType.MESH
            ),
        )

    edge = (1 - il) * (BROWS + 1)
    target = BROWS - (BROWS - 1) * il

    copies, landing = {}, {}
    for number, offset in enumerate(OFFSETS):
        di, dx, dt = offset
        side, end = (dx + 1) // 2, (dt + 1) // 2
        lanes = pl.ds(LANES * end, LANES)
        if dt == 0 and dx == 0:
            source, place = acc.at[edge], ra
        elif dt == 0:
            source, place = (corner.at[side], rc.at[side]) if di else (rims.at[side], rb.at[side])
        elif dx == 0:
            source, place = (packed_rim.at[end], re.at[end]) if di else (packed.at[end], rd.at[end])
        elif di:
            source, place = corner.at[side, :, lanes], rg.at[end, side]
        else:
            source, place = rims.at[side, :, lanes], rf.at[end, side]
        landing[offset] = place
        copies[offset] = pltpu.make_async_remote_copy(
            src_ref=source,
            dst_ref=place,
            send_sem=send_sem.at[number],
            recv_sem=recv_sem.at[number],
            device_id=device(offset),
            device_id_type=pl.DeviceIdType.MESH,
        )

    for offset in OFFSETS:
        heard = hears_from(offset)
        if heard is not None:

            def clear(place=landing[offset]):
                place[...] = jnp.zeros(place.shape, jnp.float32)

            pl.when(jnp.logical_not(heard))(clear)

    steps_copy.wait()
    wide = lax.broadcasted_iota(jnp.int32, (ROWS, SPAN), 1)
    bin_col = lax.shift_right_logical(lax.broadcasted_iota(jnp.int32, (ROWS, COLS), 1), 1) + sv[1]
    base = (sv[0] + 1) * HALF
    cbuf[...] = jnp.full(cbuf.shape, -1, jnp.int32)
    cbuf[0, :, 0:COLS] = jnp.where(
        bin_col < 0, base + LOW_RIM, jnp.where(bin_col < SPLIT, base + bin_col, -1)
    )
    cbuf[1, :, 0:COLS] = jnp.where(bin_col >= SPLIT, base + bin_col - SPLIT, -1)
    first, second = cbuf[0], cbuf[1]
    codes = (
        (
            jnp.where(wide < 120, first, -1),
            jnp.where((wide >= 120) & (wide < 240), pltpu.roll(first, 120, 1), -1),
        ),
        (
            jnp.where(wide < 104, pltpu.roll(second, SPAN - 104, 1), -1),
            jnp.where((wide >= 104) & (wide < 208), second, -1),
        ),
    )
    places = lax.broadcasted_iota(jnp.int32, (3 * HALF, SPAN), 0)
    for k in range(BROWS):
        for h in range(2):
            even, odd = codes[h]
            code = jnp.maximum(even[2 * k : 2 * k + 1], odd[2 * k + 1 : 2 * k + 2])
            chosen = jnp.where(places == code, 1.0, 0.0)
            onehot[k, h] = chosen.astype(jnp.bfloat16)
            counts = jnp.broadcast_to(jnp.sum(chosen, axis=1, keepdims=True), (3 * HALF, LANES))
            for q in range(3):
                b = k + q
                where = (b, pl.ds(HALF * h, HALF), pl.ds(SPAN, LANES))
                part = counts[HALF * q : HALF * (q + 1)]
                acc[where] = part if k == max(b - 2, 0) else acc[where] + part

    lane = lax.broadcasted_iota(jnp.int32, (8, LANES), 1)

    def in_group(r, end):
        start = (8 * r + (120 if end else 0)) % LANES
        return (lane >= start) & (lane < start + 8)

    def pack(b, end):
        tile = pl.ds(LANES * end, LANES)
        total = acc[b, 0:8, tile]
        for r in range(1, len(GROUPS)):
            turned = pltpu.roll(acc[b, GROUPS[r] : GROUPS[r] + 8, tile], 8 * r, 1)
            total = jnp.where(in_group(r, end), turned, total)
        return total

    def finish(b):
        for end in (0, 1):
            packed[end, b - 1] = pack(b, end)
        for side, row in ((0, LOW_RIM), (1, HIGH_RIM)):
            rims[side, b - 1 : b, :] = acc[b, row : row + 1, :]

    for k in range(BROWS):
        loads[k].wait()
        for h in range(2):
            start, stop = WINDOWS[h]
            pieces = [x[2 * k, start:stop, :], x[2 * k + 1, start:stop, :]]
            pieces.append(jnp.zeros((SPAN - 2 * (stop - start), SPAN), jnp.float32))
            high, low = parts_of(jnp.concatenate(pieces, axis=0))
            chosen = onehot[k, h]
            result = jnp.dot(chosen, high, preferred_element_type=jnp.float32)
            result = result + jnp.dot(chosen, low, preferred_element_type=jnp.float32)
            for q in range(3):
                b = k + q
                where = (b, pl.ds(HALF * h, HALF), pl.ds(0, SPAN))
                part = result[HALF * q : HALF * (q + 1)]
                acc[where] = part if k == max(b - 2, 0) else acc[where] + part
        if k > 0:
            finish(k)
    finish(BROWS)
    for end in (0, 1):
        packed_rim[end] = pack(edge, end)
    for side, row in ((0, LOW_RIM), (1, HIGH_RIM)):
        corner[side] = jnp.broadcast_to(acc[edge, row : row + 1, :], (8, OUT))

    beside_xl = 1 + (xl > 0).astype(jnp.int32) + (xl < n_xl - 1).astype(jnp.int32)
    beside_ta = 1 + (ta > 0).astype(jnp.int32) + (ta < n_ta - 1).astype(jnp.int32)
    pl.semaphore_wait(barrier, 2 * beside_xl * beside_ta - 1)
    for offset in sorted(OFFSETS, key=lambda o: -abs(o[2])):
        guarded(sends_to(offset), copies[offset].start)

    def heard(*offsets):
        for offset in offsets:
            guarded(hears_from(offset), copies[offset].wait_recv)

    heard((1, 0, 0), (0, -1, 0), (0, 1, 0), (1, -1, 0), (1, 1, 0))
    acc[target] = acc[target] + ra[...]
    for row, side in ((FIRST_BIN, 1), (LAST_BIN, 0)):
        acc[target, row : row + 1, :] = acc[target, row : row + 1, :] + rc[side, 0:1, :]
        for b in range(BROWS):
            acc[b + 1, row : row + 1, :] = acc[b + 1, row : row + 1, :] + rb[side, b : b + 1, :]

    table_copy.wait()

    def bins(b, tile):
        lanes = pl.ds(LANES * tile, LANES)
        return [acc[b, 0:SPLIT, lanes], acc[b, HALF : HALF + BCOLS - SPLIT, lanes]]

    def pair(p, tile):
        return jnp.concatenate(bins(2 * p + 1, tile) + bins(2 * p + 2, tile), axis=0)

    across = lax.broadcasted_iota(jnp.int32, (2 * BCOLS, LANES), 1)

    def resample(p, third, window):
        high, low = parts_of(window)
        result = jnp.dot(
            jnp.concatenate([high, low], axis=1), tab[third], preferred_element_type=jnp.float32
        )
        result = result[:, :LANES] + result[:, LANES:]
        lanes = pl.ds(LANES * third, LANES)
        out[2 * p, :, lanes] = result[:BCOLS]
        out[2 * p + 1, :, lanes] = result[BCOLS:]

    scales = []
    for p in range(BROWS // 2):
        scales.append(1.0 / jnp.maximum(pair(p, 2), 1.0))
        resample(p, 1, jnp.where(across < 64, pair(p, 1), pair(p, 0)) * scales[p])

    for end in (1, 0):
        dt = 2 * end - 1
        heard((0, 0, dt), (1, 0, dt), (0, -1, dt), (0, 1, dt), (1, -1, dt), (1, 1, dt))
        rd[end, target - 1] = rd[end, target - 1] + re[end]
        for sublane, r, side in ((0, 0, 1), (7, len(GROUPS) - 1, 0)):
            mask = in_group(r, end)
            near = jnp.where(mask, pltpu.roll(rf[end, side], 8 * r, 1) if r else rf[end, side], 0.0)
            far = jnp.where(mask, pltpu.roll(rg[end, side], 8 * r, 1) if r else rg[end, side], 0.0)
            row = slice(sublane, sublane + 1)
            rd[end, target - 1, row, :] = rd[end, target - 1, row, :] + far[0:1]
            for b in range(BROWS):
                rd[end, b, row, :] = rd[end, b, row, :] + near[b : b + 1]
        for p in range(BROWS // 2):
            halo = []
            for b in (2 * p, 2 * p + 1):
                tile = rd[end, b]
                halo += [pltpu.roll(tile, LANES - 8 * r, 1) if r else tile for r in range(len(GROUPS))]
            halo = jnp.concatenate(halo, axis=0)
            if end:
                window = jnp.where(across < 112, pair(p, 0), halo)
                resample(p, 0, window * scales[p])
            else:
                window = jnp.where(across < 16, halo, pair(p, 1))
                resample(p, 2, window * scales[p])

    for offset in OFFSETS:
        guarded(sends_to(offset), copies[offset].wait_send)


def solution(mesh):
    n_xl, n_ta = mesh.shape["xl"], mesh.shape["ta"]
    table = filter_table()
    f32 = jnp.float32

    def shards(traces, steps):
        return pl.pallas_call(
            functools.partial(kernel, n_xl, n_ta),
            name="stack_resample",
            out_shape=jax.ShapeDtypeStruct((BROWS, BCOLS, OUT), f32),
            in_specs=[pl.BlockSpec(memory_space=pltpu.HBM)] * 3,
            out_specs=pl.BlockSpec(memory_space=pltpu.VMEM),
            scratch_shapes=[
                pltpu.VMEM((ROWS, COLS, SPAN), f32),
                pltpu.VMEM((2, ROWS, COLS), jnp.int32),
                pltpu.VMEM((2, ROWS, SPAN), jnp.int32),
                pltpu.VMEM((3, SPAN, SPAN), jnp.bfloat16),
                pltpu.VMEM((BROWS, 2, 3 * HALF, SPAN), jnp.bfloat16),
                pltpu.VMEM((BROWS + 2, 2 * HALF, OUT), f32),
                pltpu.VMEM((2, BROWS, OUT), f32),
                pltpu.VMEM((2, 8, OUT), f32),
                pltpu.VMEM((2, BROWS, 8, LANES), f32),
                pltpu.VMEM((2, 8, LANES), f32),
                pltpu.VMEM((2 * HALF, OUT), f32),
                pltpu.VMEM((2, BROWS, OUT), f32),
                pltpu.VMEM((2, 8, OUT), f32),
                pltpu.VMEM((2, BROWS, 8, LANES), f32),
                pltpu.VMEM((2, 8, LANES), f32),
                pltpu.VMEM((2, 2, BROWS, LANES), f32),
                pltpu.VMEM((2, 2, 8, LANES), f32),
                pltpu.SemaphoreType.DMA((BROWS + 2,)),
                pltpu.SemaphoreType.DMA((len(OFFSETS),)),
                pltpu.SemaphoreType.DMA((len(OFFSETS),)),
            ],
            compiler_params=pltpu.CompilerParams(
                collective_id=0, has_side_effects=True, vmem_limit_bytes=32 * 1024 * 1024
            ),
        )(traces, steps, table)

    return jax.shard_map(
        shards,
        mesh=mesh,
        in_specs=(P("il", "xl", "ta"), P(None, "il", "xl")),
        out_specs=P("il", "xl", "ta"),
        check_vma=False,
    )
```

time: 97.7 us -> 18.4 us (0.19)
  the two profiles are of different devices: /device:TPU:126 before, /device:TPU:227 now
where the time goes in v1:
time: 18.4 us; the launch traced here: 18.2 us
  Pallas kernels  13.4 us (73%)
  local copies, waits for them, and re-layouts  4.76 us (26%)
    pallas_call x1, Pallas kernels, shards(): pl.pallas_call(functools.partial(kernel, n_xl, n_ta), name='stack_resampl...  13.4 us
    unnamed x7, local copies, waits for them, and re-layouts  4.76 us

profile of v1, /device:TPU:227, one launch (start us, length us, event | category | flops | bytes accessed | tf_op | source)
XLA Modules:
  0.0 18.2 jit_solution(7293333101897979716)
XLA Ops:
  0.0 0.0 copy-start
  0.0 2.0 %copy-done = f32[16,208,256]{2,1,0:T(8,128)S(1)} copy-done((f32[16,208,256]{2,1,0:T(8,128)S(1)}, f32[16,208,256]{2,1,0:T(8,128)}, u32[]{:S(2)}) %copy-start) | copy-done | bytes 3407896
  2.0 0.0 copy-start.1
  2.0 1.0 %copy-done.1 = bf16[3,256,256]{2,1,0:T(8,128)(2,1)S(1)} copy-done((bf16[3,256,256]{2,1,0:T(8,128)(2,1)S(1)}, bf16[3,256,256]{2,1,0:T(8,128)(2,1)}, u32[]{:S(2)}) %copy-start.1) | copy-done | bytes 393240
  3.0 0.0 copy-start.2
  3.0 0.8 %copy-done.2 = s32[2,16,208]{2,1,0:T(8,128)S(1)} copy-done((s32[2,16,208]{2,1,0:T(8,128)S(1)}, s32[2,16,208]{2,1,0:T(8,128)}, u32[]{:S(2)}) %copy-start.2) | copy-done | bytes 26648
  3.7 13.4 %stack_resample.1 = f32[8,104,384]{2,1,0:T(8,128)S(1)} custom-call(f32[16,208,256]{2,1,0:T(8,128)S(1)} %copy-done, s32[2,16,208]{2,1,0:T(8,128)S(1)} %copy-done.2, bf16[3,256,256]{2,1,0:T(8,128)(2,1)S(1)} %copy-done.1), custom_call_target="tpu_custom_call" | custom-call | tf_op jit(solution)/shard_map/stack_resample/pallas_call | solution.py:298
  17.1 1.0 %copy.5 = f32[8,104,384]{2,1,0:T(8,128)} copy(f32[8,104,384]{2,1,0:T(8,128)S(1)} %stack_resample.1) | data formatting | bytes 2555904
Async XLA Ops:
  0.0 2.0 %copy-start = (f32[16,208,256]{2,1,0:T(8,128)S(1)}, f32[16,208,256]{2,1,0:T(8,128)}, u32[]{:S(2)}) copy-start(f32[16,208,256]{2,1,0:T(8,128)} %traces.1) | copy-start | bytes 10223620
  2.0 1.0 %copy-start.1 = (bf16[3,256,256]{2,1,0:T(8,128)(2,1)S(1)}, bf16[3,256,256]{2,1,0:T(8,128)(2,1)}, u32[]{:S(2)}) copy-start(bf16[3,256,256]{2,1,0:T(8,128)(2,1)} %constant.2.clone.table) | copy-start | bytes 1179652
  3.0 0.8 %copy-start.2 = (s32[2,16,208]{2,1,0:T(8,128)S(1)}, s32[2,16,208]{2,1,0:T(8,128)}, u32[]{:S(2)}) copy-start(s32[2,16,208]{2,1,0:T(8,128)} %steps.1) | copy-start | bytes 79876

commit v2 on v1

--- a/solution.py
+++ b/solution.py
@@ -326,7 +326,7 @@
             compiler_params=pltpu.CompilerParams(
                 collective_id=0, has_side_effects=True, vmem_limit_bytes=32 * 1024 * 1024
             ),
-        )(traces, steps, table)
+        )(*(pltpu.with_memory_space_constraint(a, pltpu.HBM) for a in (traces, steps, jnp.asarray(table))))
 
     return jax.shard_map(
         shards,

time: 18.4 us -> 13 us (0.71); the launches traced: 18.2 us -> 13 us
  local copies, waits for them, and re-layouts: 4.76 us -> 1.05 us
  Pallas kernels: 13.4 us -> 11.9 us
    unnamed x7 -> x1, local copies, waits for them, and re-layouts: 4.76 us -> 1.05 us
    pallas_call x1, Pallas kernels: 13.4 us -> 11.9 us  [shards(): pl.pallas_call(functools.partial(kernel, n_xl, n_ta), name='stack_resampl...]
where the time goes in v2:
time: 13 us
  Pallas kernels  11.9 us (92%)
  local copies, waits for them, and re-layouts  1.05 us (8%)
    pallas_call x1, Pallas kernels, shards(): pl.pallas_call(functools.partial(kernel, n_xl, n_ta), name='stack_resampl...  11.9 us
    unnamed x1, local copies, waits for them, and re-layouts  1.05 us

profile of v2, /device:TPU:227, one launch (start us, length us, event | category | flops | bytes accessed | tf_op | source)
XLA Modules:
  0.0 13.0 jit_solution(757924792448345944)
XLA Ops:
  0.0 11.9 %stack_resample.1 = f32[8,104,384]{2,1,0:T(8,128)S(1)} custom-call(f32[16,208,256]{2,1,0:T(8,128)} %traces.1, s32[2,16,208]{2,1,0:T(8,128)} %steps.1, bf16[3,256,256]{2,1,0:T(8,128)(2,1)} %constant.2.clone.table), custom_call_target="tpu_custom_call" | custom-call | tf_op jit(solution)/shard_map/stack_resample/pallas_call | solution.py:298
  11.9 1.0 %copy.5 = f32[8,104,384]{2,1,0:T(8,128)} copy(f32[8,104,384]{2,1,0:T(8,128)S(1)} %stack_resample.1) | data formatting | bytes 2555904

commit v3 on v2

v3 whole, which is shorter than its diff:
```python
import functools

import jax
import jax.numpy as jnp
import numpy as np
from jax import lax
from jax.experimental import pallas as pl
from jax.experimental.pallas import tpu as pltpu
from jax.sharding import PartitionSpec as P

TAPS = 16
P_SIZE = 3
Q = 2
REACH = TAPS // 2

LANES = 128
ROWS, COLS, SPAN = 16, 208, 256
BROWS, BCOLS, OUT = 8, 104, 384
HALF = 64
SPLIT = 56
LOW_RIM, HIGH_RIM = 56, 112
FIRST_BIN, LAST_BIN = 0, 111
WINDOWS = ((0, 120), (104, 208))
GROUPS = tuple(range(0, 56, 8)) + tuple(range(64, 112, 8))

OFFSETS = tuple(
    (di, dx, dt) for di in (0, 1) for dx in (-1, 0, 1) for dt in (-1, 0, 1) if (di, dx, dt) != (0, 0, 0)
)


SIDES = ((-1, -1), (-1, 1), (1, -1), (1, 1), (0, -1), (0, 1), (-1, 0), (1, 0), (0, 0))


def filter_table():
    lane = np.arange(LANES)
    sample = np.stack(
        [
            np.where(lane < 112, lane, lane - 128),
            np.where(lane < 64, lane + 128, lane),
            np.where(lane < 16, lane + 256, lane + 128),
        ]
    )
    output = np.arange(OUT).reshape(3, LANES)
    x = (Q * output[:, None, :] - P_SIZE * sample[:, :, None]) / P_SIZE
    weights = np.where(np.abs(x) < REACH, np.sinc(x) * np.sinc(x / REACH), 0.0).astype(np.float32)
    high = weights.astype(jnp.bfloat16)
    low = (weights - high.astype(np.float32)).astype(jnp.bfloat16)
    top = np.concatenate([high, low], axis=2)
    bottom = np.concatenate([high, np.zeros_like(low)], axis=2)
    return np.concatenate([top, bottom], axis=1)


def parts_of(values):
    high = values.astype(jnp.bfloat16)
    low = (values - high.astype(jnp.float32)).astype(jnp.bfloat16)
    return high, low


def both(*conditions):
    held = [c for c in conditions if c is not None]
    return functools.reduce(jnp.logical_and, held) if held else None


def kernel(
    n_xl, n_ta, traces, steps, table, out,
    x, sv, cbuf, tab, onehot, acc, scale, rims, corner, packed, packed_rim,
    ra, rb, rc, rd, re, rf, rg, load_sem, send_sem, recv_sem,
):
    il, xl, ta = lax.axis_index("il"), lax.axis_index("xl"), lax.axis_index("ta")

    def there(step, index, size):
        return None if step == 0 else (index > 0 if step < 0 else index < size - 1)

    def device(offset):
        return {"il": 1 - il if offset[0] else il, "xl": xl + offset[1], "ta": ta + offset[2]}

    def for_neighbours(sides, action, sign=1):
        for dx, dt in sides:
            condition = both(there(sign * dx, xl, n_xl), there(sign * dt, ta, n_ta))

            def run(dx=dx, dt=dt):
                for di in (0, 1):
                    if (di, dx, dt) != (0, 0, 0):
                        action((di, dx, dt))

            if condition is None:
                run()
            else:
                pl.when(condition)(run)

    barrier = pltpu.get_barrier_semaphore()

    def greet(offset):
        pl.semaphore_signal(
            barrier, 1, device_id=device(offset), device_id_type=pl.DeviceIdType.MESH
        )

    for_neighbours(SIDES, greet)

    steps_copy = pltpu.make_async_copy(steps, sv, load_sem.at[0])
    steps_copy.start()
    loads = []
    for k in range(BROWS):
        rows = pl.ds(2 * k, 2)
        loads.append(pltpu.make_async_copy(traces.at[rows], x.at[rows], load_sem.at[k + 1]))
        loads[-1].start()
    table_copy = pltpu.make_async_copy(table, tab, load_sem.at[BROWS + 1])
    table_copy.start()

    edge = (1 - il) * (BROWS + 1)
    target = BROWS - (BROWS - 1) * il

    copies = {}
    for number, offset in enumerate(OFFSETS):
        di, dx, dt = offset
        side, end = (dx + 1) // 2, (dt + 1) // 2
        lanes = pl.ds(LANES * end, LANES)
        if dt == 0 and dx == 0:
            rows = pl.ds(0, LAST_BIN + 1)
            source, place = acc.at[edge, rows], ra
        elif dt == 0:
            source, place = (corner.at[side], rc.at[side]) if di else (rims.at[side], rb.at[side])
        elif dx == 0:
            source, place = (packed_rim.at[end], re.at[end]) if di else (packed.at[end], rd.at[end])
        elif di:
            source, place = corner.at[side, :, lanes], rg.at[end, side]
        else:
            source, place = rims.at[side, :, lanes], rf.at[end, side]
        copies[offset] = pltpu.make_async_remote_copy(
            src_ref=source,
            dst_ref=place,
            send_sem=send_sem.at[number],
            recv_sem=recv_sem.at[number],
            device_id=device(offset),
            device_id_type=pl.DeviceIdType.MESH,
        )

    for dx in (-1, 1):
        side = (dx + 1) // 2

        @pl.when(jnp.logical_not(there(-dx, xl, n_xl)))
        def _(side=side):
            for place in (rb.at[side], rc.at[side], *(r.at[e, side] for r in (rf, rg) for e in (0, 1))):
                place[...] = jnp.zeros(place.shape, jnp.float32)

    for dt in (-1, 1):
        end = (dt + 1) // 2

        @pl.when(jnp.logical_not(there(-dt, ta, n_ta)))
        def _(end=end):
            for place in (rd.at[end], re.at[end], rf.at[end], rg.at[end]):
                place[...] = jnp.zeros(place.shape, jnp.float32)

    steps_copy.wait()
    wide = lax.broadcasted_iota(jnp.int32, (ROWS, SPAN), 1)
    bin_col = lax.shift_right_logical(lax.broadcasted_iota(jnp.int32, (ROWS, COLS), 1), 1) + sv[1]
    base = (sv[0] + 1) * HALF
    cbuf[...] = jnp.full(cbuf.shape, -1, jnp.int32)
    cbuf[0, :, 0:COLS] = jnp.where(
        bin_col < 0, base + LOW_RIM, jnp.where(bin_col < SPLIT, base + bin_col, -1)
    )
    cbuf[1, :, 0:COLS] = jnp.where(bin_col >= SPLIT, base + bin_col - SPLIT, -1)
    first, second = cbuf[0], cbuf[1]
    codes = (
        (
            jnp.where(wide < 120, first, -1),
            jnp.where((wide >= 120) & (wide < 240), pltpu.roll(first, 120, 1), -1),
        ),
        (
            jnp.where(wide < 104, pltpu.roll(second, SPAN - 104, 1), -1),
            jnp.where((wide >= 104) & (wide < 208), second, -1),
        ),
    )
    places = lax.broadcasted_iota(jnp.int32, (3 * HALF, SPAN), 0)
    for k in range(BROWS):
        for h in range(2):
            even, odd = codes[h]
            code = jnp.maximum(even[2 * k : 2 * k + 1], odd[2 * k + 1 : 2 * k + 2])
            onehot[k, h] = jnp.where(places == code, 1.0, 0.0).astype(jnp.bfloat16)

    for b in range(BROWS + 2):
        for h in range(2):
            rows = [onehot[k, h, HALF * (b - k) : HALF * (b - k + 1), :] for k in range(BROWS) if 0 <= b - k < 3]
            total = functools.reduce(jnp.add, rows)
            total = (total[:, :LANES] + total[:, LANES:]).astype(jnp.float32)
            acc[b, HALF * h : HALF * (h + 1), SPAN:OUT] = jnp.broadcast_to(
                jnp.sum(total, axis=1, keepdims=True), (HALF, LANES)
            )

    lane = lax.broadcasted_iota(jnp.int32, (8, LANES), 1)
    sublane = lax.broadcasted_iota(jnp.int32, (8, LANES), 0)

    def in_group(r, end):
        start = (8 * r + (120 if end else 0)) % LANES
        return (lane >= start) & (lane < start + 8)

    def pack(b, end):
        tile = pl.ds(LANES * end, LANES)
        total = acc[b, 0:8, tile]
        for r in range(1, len(GROUPS)):
            turned = pltpu.roll(acc[b, GROUPS[r] : GROUPS[r] + 8, tile], 8 * r, 1)
            total = jnp.where(in_group(r, end), turned, total)
        return total

    def finish(b):
        for side, row in ((0, LOW_RIM), (1, HIGH_RIM)):
            rims[side, b - 1 : b, :] = acc[b, row : row + 1, :]
        for end in (0, 1):
            packed[end, b - 1] = pack(b, end)

    for block in (range(0, 4), range(4, 8)):
        for k in block:
            loads[k].wait()
        for k in block:
            for h in range(2):
                start, stop = WINDOWS[h]
                pieces = [x[2 * k, start:stop, :], x[2 * k + 1, start:stop, :]]
                pieces.append(jnp.zeros((SPAN - 2 * (stop - start), SPAN), jnp.float32))
                high, low = parts_of(jnp.concatenate(pieces, axis=0))
                chosen = onehot[k, h]
                result = jnp.dot(chosen, high, preferred_element_type=jnp.float32)
                result = result + jnp.dot(chosen, low, preferred_element_type=jnp.float32)
                for q in range(3):
                    b = k + q
                    where = (b, pl.ds(HALF * h, HALF), pl.ds(0, SPAN))
                    part = result[HALF * q : HALF * (q + 1)]
                    acc[where] = part if k == max(b - 2, 0) else acc[where] + part
            if k > 0:
                finish(k)
    finish(BROWS)
    for side, row in ((0, LOW_RIM), (1, HIGH_RIM)):
        corner[side] = acc[edge, row : row + 1, :]
    for end in (0, 1):
        packed_rim[end] = pack(edge, end)

    beside_xl = 1 + (xl > 0).astype(jnp.int32) + (xl < n_xl - 1).astype(jnp.int32)
    beside_ta = 1 + (ta > 0).astype(jnp.int32) + (ta < n_ta - 1).astype(jnp.int32)
    pl.semaphore_wait(barrier, 2 * beside_xl * beside_ta - 1)
    for_neighbours(SIDES, lambda offset: copies[offset].start())

    for_neighbours(SIDES[6:], lambda offset: copies[offset].wait_recv(), -1)
    acc[target, 0 : LAST_BIN + 1, :] = acc[target, 0 : LAST_BIN + 1, :] + ra[...]
    for row, side in ((FIRST_BIN, 1), (LAST_BIN, 0)):
        acc[target, row : row + 1, :] = acc[target, row : row + 1, :] + rc[side]
        for b in range(BROWS):
            acc[b + 1, row : row + 1, :] = acc[b + 1, row : row + 1, :] + rb[side, b : b + 1, :]

    table_copy.wait()

    def bins(b, tile):
        lanes = pl.ds(LANES * tile, LANES)
        return [acc[b, 0:SPLIT, lanes], acc[b, HALF : HALF + BCOLS - SPLIT, lanes]]

    def pair(p, tile):
        return jnp.concatenate(bins(2 * p + 1, tile) + bins(2 * p + 2, tile), axis=0)

    across = lax.broadcasted_iota(jnp.int32, (2 * BCOLS, LANES), 1)

    def resample(p, third, window):
        high, low = parts_of(window)
        result = jnp.dot(
            jnp.concatenate([high, low], axis=1), tab[third], preferred_element_type=jnp.float32
        )
        result = result[:, :LANES] + result[:, LANES:]
        lanes = pl.ds(LANES * third, LANES)
        out[2 * p, :, lanes] = result[:BCOLS]
        out[2 * p + 1, :, lanes] = result[BCOLS:]

    for p in range(BROWS // 2):
        scale[p] = 1.0 / jnp.maximum(pair(p, 2), 1.0)
        resample(p, 1, jnp.where(across < 64, pair(p, 1), pair(p, 0)) * scale[p])

    for_neighbours(SIDES[:6], lambda offset: copies[offset].wait_recv(), -1)

    def halo(end):
        last = len(GROUPS) - 1
        here = in_group(0, end), in_group(last, end)
        near = [jnp.where(here[0], rf[end, 1], 0.0), jnp.where(here[1], pltpu.roll(rf[end, 0], 8 * last, 1), 0.0)]
        far = jnp.where(here[0] & (sublane == 0), rg[end, 1], 0.0)
        turned = pltpu.roll(jnp.broadcast_to(rg[end, 0], (8, LANES)), 8 * last, 1)
        far = far + jnp.where(here[1] & (sublane == 7), turned, 0.0) + re[end]
        rows = []
        for b in range(BROWS):
            tile = rd[end, b]
            tile = tile + jnp.where(sublane == 0, near[0][b : b + 1], 0.0)
            tile = tile + jnp.where(sublane == 7, near[1][b : b + 1], 0.0)
            if b in (0, BROWS - 1):
                tile = tile + jnp.where(target == b + 1, far, 0.0)
            rows += [pltpu.roll(tile, LANES - 8 * r, 1) if r else tile for r in range(len(GROUPS))]
        return rows

    before, after = halo(1), halo(0)
    per = 2 * len(GROUPS)
    for p in range(BROWS // 2):
        window = jnp.where(across < 112, pair(p, 0), jnp.concatenate(before[per * p : per * (p + 1)], axis=0))
        resample(p, 0, window * scale[p])
        window = jnp.where(across < 16, jnp.concatenate(after[per * p : per * (p + 1)], axis=0), pair(p, 1))
        resample(p, 2, window * scale[p])

    for_neighbours(SIDES, lambda offset: copies[offset].wait_send())


def solution(mesh):
    n_xl, n_ta = mesh.shape["xl"], mesh.shape["ta"]
    table = filter_table()
    f32 = jnp.float32

    def shards(traces, steps):
        return pl.pallas_call(
            functools.partial(kernel, n_xl, n_ta),
            name="stack_resample",
            out_shape=jax.ShapeDtypeStruct((BROWS, BCOLS, OUT), f32),
            in_specs=[pl.BlockSpec(memory_space=pltpu.HBM)] * 3,
            out_specs=pl.BlockSpec(memory_space=pltpu.VMEM),
            scratch_shapes=[
                pltpu.VMEM((ROWS, COLS, SPAN), f32),
                pltpu.VMEM((2, ROWS, COLS), jnp.int32),
                pltpu.VMEM((2, ROWS, SPAN), jnp.int32),
                pltpu.VMEM((3, SPAN, SPAN), jnp.bfloat16),
                pltpu.VMEM((BROWS, 2, 3 * HALF, SPAN), jnp.bfloat16),
                pltpu.VMEM((BROWS + 2, 2 * HALF, OUT), f32),
                pltpu.VMEM((BROWS // 2, 2 * BCOLS, LANES), f32),
                pltpu.VMEM((2, BROWS, OUT), f32),
                pltpu.VMEM((2, 1, OUT), f32),
                pltpu.VMEM((2, BROWS, 8, LANES), f32),
                pltpu.VMEM((2, 8, LANES), f32),
                pltpu.VMEM((LAST_BIN + 1, OUT), f32),
                pltpu.VMEM((2, BROWS, OUT), f32),
                pltpu.VMEM((2, 1, OUT), f32),
                pltpu.VMEM((2, BROWS, 8, LANES), f32),
                pltpu.VMEM((2, 8, LANES), f32),
                pltpu.VMEM((2, 2, BROWS, LANES), f32),
                pltpu.VMEM((2, 2, 1, LANES), f32),
                pltpu.SemaphoreType.DMA((BROWS + 2,)),
                pltpu.SemaphoreType.DMA((len(OFFSETS),)),
                pltpu.SemaphoreType.DMA((len(OFFSETS),)),
            ],
            compiler_params=pltpu.CompilerParams(
                collective_id=0, has_side_effects=True, vmem_limit_bytes=32 * 1024 * 1024
            ),
        )(*(pltpu.with_memory_space_constraint(a, pltpu.HBM) for a in (traces, steps, jnp.asarray(table))))

    return jax.shard_map(
        shards,
        mesh=mesh,
        in_specs=(P("il", "xl", "ta"), P(None, "il", "xl")),
        out_specs=P("il", "xl", "ta"),
        check_vma=False,
    )
```

time: 13 us -> 11.4 us (0.88)
  Pallas kernels: 11.9 us -> 10.2 us
    pallas_call x1, Pallas kernels: 11.9 us -> 10.2 us  [shards(): pl.pallas_call(functools.partial(kernel, n_xl, n_ta), name='stack_resampl...]
where the time goes in v3:
time: 11.4 us; the launch traced here: 11.3 us
  Pallas kernels  10.2 us (89%)
  local copies, waits for them, and re-layouts  1.05 us (9%)
    pallas_call x1, Pallas kernels, shards(): pl.pallas_call(functools.partial(kernel, n_xl, n_ta), name='stack_resampl...  10.2 us
    unnamed x1, local copies, waits for them, and re-layouts  1.05 us

profile of v3, /device:TPU:227, one launch (start us, length us, event | category | flops | bytes accessed | tf_op | source)
XLA Modules:
  0.0 11.3 jit_solution(10875418111918109558)
XLA Ops:
  0.0 10.2 %stack_resample.1 = f32[8,104,384]{2,1,0:T(8,128)S(1)} custom-call(f32[16,208,256]{2,1,0:T(8,128)} %traces.1, s32[2,16,208]{2,1,0:T(8,128)} %steps.1, bf16[3,256,256]{2,1,0:T(8,128)(2,1)} %constant.2.clone.table), custom_call_target="tpu_custom_call" | custom-call | tf_op jit(solution)/shard_map/stack_resample/pallas_call | solution.py:309
  10.2 1.0 %copy.5 = f32[8,104,384]{2,1,0:T(8,128)} copy(f32[8,104,384]{2,1,0:T(8,128)S(1)} %stack_resample.1) | data formatting | bytes 2555904

commit v4 on v3

v4 whole, which is shorter than its diff:
```python
import functools

import jax
import jax.numpy as jnp
import numpy as np
from jax import lax
from jax.experimental import pallas as pl
from jax.experimental.pallas import tpu as pltpu
from jax.sharding import PartitionSpec as P

TAPS = 16
P_SIZE = 3
Q = 2
REACH = TAPS // 2

LANES = 128
ROWS, COLS, SPAN = 16, 208, 256
BROWS, BCOLS, OUT = 8, 104, 384
HALVES = (64, 48)
STARTS = (0, 64)
HELD = 112
SPLIT = 56
FIRST_BIN, LAST_BIN = 0, 111
WINDOWS = ((0, 120), (104, 208))
GROUPS = tuple(range(0, 56, 8)) + tuple(range(64, 112, 8))

OFFSETS = tuple(
    (di, dx, dt) for di in (0, 1) for dx in (-1, 0, 1) for dt in (-1, 0, 1) if (di, dx, dt) != (0, 0, 0)
)


SIDES = ((-1, -1), (-1, 1), (1, -1), (1, 1), (0, -1), (0, 1), (-1, 0), (1, 0), (0, 0))
EARLY = SIDES[:4] + SIDES[6:8]
LATE = SIDES[4:6] + SIDES[8:]
BLOCKS = (range(0, 4), range(4, 8))


def filter_table():
    lane = np.arange(LANES)
    sample = np.stack(
        [
            np.where(lane < 112, lane, lane - 128),
            np.where(lane < 64, lane + 128, lane),
            np.where(lane < 16, lane + 256, lane + 128),
        ]
    )
    output = np.arange(OUT).reshape(3, LANES)
    x = (Q * output[:, None, :] - P_SIZE * sample[:, :, None]) / P_SIZE
    weights = np.where(np.abs(x) < REACH, np.sinc(x) * np.sinc(x / REACH), 0.0).astype(np.float32)
    high = weights.astype(jnp.bfloat16)
    low = (weights - high.astype(np.float32)).astype(jnp.bfloat16)
    top = np.concatenate([high, low], axis=2)
    bottom = np.concatenate([high, np.zeros_like(low)], axis=2)
    return np.concatenate([top, bottom], axis=1)


def halo_table():
    sample = np.arange(8)[:, None]
    weights = np.zeros((2, LANES, SPAN), np.float32)
    for end in (0, 1):
        n = sample - 8 if end else sample + SPAN
        x = (Q * (np.arange(16)[None, :] + (0 if end else OUT - 16)) - P_SIZE * n) / P_SIZE
        part = np.where(np.abs(x) < REACH, np.sinc(x) * np.sinc(x / REACH), 0.0)
        for r in range(len(GROUPS)):
            first = (8 * r + 120 * end) % LANES
            weights[end, first : first + 8, 16 * r : 16 * (r + 1)] = part
    high = weights.astype(jnp.bfloat16)
    low = (weights - high.astype(np.float32)).astype(jnp.bfloat16)
    return np.stack(
        [np.concatenate([high, high], axis=1), np.concatenate([low, np.zeros_like(low)], axis=1)], axis=1
    )


def parts_of(values):
    high = values.astype(jnp.bfloat16)
    low = (values - high.astype(jnp.float32)).astype(jnp.bfloat16)
    return high, low


def both(*conditions):
    held = [c for c in conditions if c is not None]
    return functools.reduce(jnp.logical_and, held) if held else None


def kernel(
    load_sem, send_sem, n_xl, n_ta, traces, steps, table, ends_table, out,
    x, edges, sv, cbuf, tab, tab_ends, onehot0, onehot1, acc, scale_packed, rims, packed, packed_rim,
    ra, rb, rc, rd, re, rf, rg, recv_sem,
):
    il, xl, ta = lax.axis_index("il"), lax.axis_index("xl"), lax.axis_index("ta")

    def there(step, index, size):
        return None if step == 0 else (index > 0 if step < 0 else index < size - 1)

    def device(offset):
        return {"il": 1 - il if offset[0] else il, "xl": xl + offset[1], "ta": ta + offset[2]}

    def for_neighbours(sides, action, sign=1):
        for dx, dt in sides:
            condition = both(there(sign * dx, xl, n_xl), there(sign * dt, ta, n_ta))

            def run(dx=dx, dt=dt):
                for di in (0, 1):
                    if (di, dx, dt) != (0, 0, 0):
                        action((di, dx, dt))

            if condition is None:
                run()
            else:
                pl.when(condition)(run)

    barrier = pltpu.get_barrier_semaphore()

    def greet(offset):
        pl.semaphore_signal(
            barrier, 1, device_id=device(offset), device_id_type=pl.DeviceIdType.MESH
        )

    for_neighbours(SIDES, greet)

    steps_copy = pltpu.make_async_copy(steps, sv, load_sem.at[0])
    steps_copy.start()
    edge_copies = []
    for side in (0, 1):
        columns = pl.ds((COLS - 8) * side, 8)
        edge_copies.append(pltpu.make_async_copy(traces.at[:, columns, :], edges.at[side], load_sem.at[1 + side]))
        edge_copies[-1].start()
    loads = []
    for block in BLOCKS:
        rows = pl.ds(2 * block[0], 2 * len(block))
        loads.append(pltpu.make_async_copy(traces.at[rows], x.at[rows], load_sem.at[3 + len(loads)]))
        loads[-1].start()
    table_copies = [
        pltpu.make_async_copy(table, tab, load_sem.at[3 + len(BLOCKS)]),
        pltpu.make_async_copy(ends_table, tab_ends, load_sem.at[4 + len(BLOCKS)]),
    ]
    for copy in table_copies:
        copy.start()

    edge = (1 - il) * (BROWS + 1)
    target = BROWS - (BROWS - 1) * il

    own, far = pl.ds(0, BROWS), pl.ds(BROWS, 1)
    copies = {}
    for number, offset in enumerate(OFFSETS):
        di, dx, dt = offset
        side, end = (dx + 1) // 2, (dt + 1) // 2
        lanes = pl.ds(LANES * end, LANES)
        if dt == 0 and dx == 0:
            source, place = acc.at[edge], ra
        elif dt == 0:
            source, place = (rims.at[side, far], rc.at[side]) if di else (rims.at[side, own], rb.at[side])
        elif dx == 0:
            source, place = (packed_rim.at[end], re.at[end]) if di else (packed.at[end], rd.at[end])
        elif di:
            source, place = rims.at[side, far, lanes], rg.at[end, side]
        else:
            source, place = rims.at[side, own, lanes], rf.at[end, side]
        copies[offset] = pltpu.make_async_remote_copy(
            src_ref=source,
            dst_ref=place,
            send_sem=send_sem.at[number],
            recv_sem=recv_sem.at[number],
            device_id=device(offset),
            device_id_type=pl.DeviceIdType.MESH,
        )

    for dx in (-1, 1):
        side = (dx + 1) // 2

        @pl.when(jnp.logical_not(there(-dx, xl, n_xl)))
        def _(side=side):
            for place in (rb.at[side], rc.at[side], *(r.at[e, side] for r in (rf, rg) for e in (0, 1))):
                place[...] = jnp.zeros(place.shape, jnp.float32)

    for dt in (-1, 1):
        end = (dt + 1) // 2

        @pl.when(jnp.logical_not(there(-dt, ta, n_ta)))
        def _(end=end):
            for place in (rd.at[end], re.at[end], rf.at[end], rg.at[end]):
                place[...] = jnp.zeros(place.shape, jnp.float32)

    steps_copy.wait()
    row_bin = lax.shift_right_logical(lax.broadcasted_iota(jnp.int32, (ROWS, COLS), 0), 1) + sv[0]
    inside = (row_bin >= 0) & (row_bin < BROWS)
    row_code = jnp.where(inside, row_bin, jnp.where(row_bin == edge - 1, BROWS, -1))
    wide = lax.broadcasted_iota(jnp.int32, (ROWS, SPAN), 1)
    bin_col = lax.shift_right_logical(lax.broadcasted_iota(jnp.int32, (ROWS, COLS), 1), 1) + sv[1]
    cbuf[...] = jnp.full(cbuf.shape, -1, jnp.int32)
    cbuf[0, :, 0:COLS] = jnp.where(
        (bin_col >= 0) & (bin_col < SPLIT), (sv[0] + 1) * HALVES[0] + bin_col, -1
    )
    cbuf[1, :, 0:COLS] = jnp.where(
        (bin_col >= SPLIT) & (bin_col < BCOLS), (sv[0] + 1) * HALVES[1] + bin_col - SPLIT, -1
    )
    first, second = cbuf[0], cbuf[1]
    codes = (
        (
            jnp.where(wide < 120, first, -1),
            jnp.where((wide >= 120) & (wide < 240), pltpu.roll(first, 120, 1), -1),
        ),
        (
            jnp.where(wide < 104, pltpu.roll(second, SPAN - 104, 1), -1),
            jnp.where((wide >= 104) & (wide < 208), second, -1),
        ),
    )
    onehot = (onehot0, onehot1)
    for h, size in enumerate(HALVES):
        places = lax.broadcasted_iota(jnp.int32, (3 * size, SPAN), 0)
        even, odd = codes[h]
        for k in range(BROWS):
            code = jnp.maximum(even[2 * k : 2 * k + 1], odd[2 * k + 1 : 2 * k + 2])
            onehot[h][k] = jnp.where(places == code, 1.0, 0.0).astype(jnp.bfloat16)

    for b in range(BROWS + 2):
        for h, size in enumerate(HALVES):
            rows = [onehot[h][k, size * (b - k) : size * (b - k + 1), :] for k in range(BROWS) if 0 <= b - k < 3]
            total = functools.reduce(jnp.add, rows)
            total = (total[:, :LANES] + total[:, LANES:]).astype(jnp.float32)
            acc[b, STARTS[h] : STARTS[h] + size, SPAN:OUT] = jnp.broadcast_to(
                jnp.sum(total, axis=1, keepdims=True), (size, LANES)
            )

    lane = lax.broadcasted_iota(jnp.int32, (8, LANES), 1)
    sublane = lax.broadcasted_iota(jnp.int32, (8, LANES), 0)

    def in_group(r, end):
        start = (8 * r + (120 if end else 0)) % LANES
        return (lane >= start) & (lane < start + 8)

    def pack(b, end):
        tile = pl.ds(LANES * end, LANES)
        total = acc[b, 0:8, tile]
        for r in range(1, len(GROUPS)):
            turned = pltpu.roll(acc[b, GROUPS[r] : GROUPS[r] + 8, tile], 8 * r, 1)
            total = jnp.where(in_group(r, end), turned, total)
        return total

    def send(offset):
        copies[offset].start()

    def find_rims():
        slots = lax.broadcasted_iota(jnp.int32, (ROWS, 2 * BROWS), 1)
        ones = jnp.ones((2 * ROWS, LANES), jnp.float32)
        for side in (0, 1):
            code = jnp.where(sv[1] == 2 * side - 1, row_code, -1)
            chosen, values = [], []
            for j in (0, 1):
                column = (COLS - 2) * side + j
                chosen.append(jnp.where(slots == code[:, column : column + 1], 1.0, 0.0))
                values.append(edges[side, :, 6 * side + j, :])
            rims[side] = lax.dot_general(
                jnp.concatenate(chosen, axis=0),
                jnp.concatenate([jnp.concatenate(values, axis=0), ones], axis=1),
                (((0,), (0,)), ((), ())),
                precision=lax.Precision.HIGHEST,
                preferred_element_type=jnp.float32,
            )

    distant = (lax.rem(ta, 4) == 0) | (ta == n_ta // 2 - 1)

    def meet():
        beside_xl = 1 + (xl > 0).astype(jnp.int32) + (xl < n_xl - 1).astype(jnp.int32)
        beside_ta = 1 + (ta > 0).astype(jnp.int32) + (ta < n_ta - 1).astype(jnp.int32)
        pl.semaphore_wait(barrier, 2 * beside_xl * beside_ta - 1)

    for block, load in zip(BLOCKS, loads):
        load.wait()
        if block is BLOCKS[0]:
            for copy in edge_copies:
                copy.wait()
            find_rims()
        for k in block:
            for h, size in enumerate(HALVES):
                start, stop = WINDOWS[h]
                pieces = [x[2 * k, start:stop, :], x[2 * k + 1, start:stop, :]]
                pieces.append(jnp.zeros((SPAN - 2 * (stop - start), SPAN), jnp.float32))
                high, low = parts_of(jnp.concatenate(pieces, axis=0))
                chosen = onehot[h][k]
                result = jnp.dot(chosen, high, preferred_element_type=jnp.float32)
                result = result + jnp.dot(chosen, low, preferred_element_type=jnp.float32)
                for q in range(3):
                    b = k + q
                    where = (b, pl.ds(STARTS[h], size), pl.ds(0, SPAN))
                    part = result[size * q : size * (q + 1)]
                    acc[where] = part if k == max(b - 2, 0) else acc[where] + part
            if k > 0:
                for end in (0, 1):
                    packed[end, k - 1] = pack(k, end)
        if block is BLOCKS[0]:

            @pl.when(jnp.logical_not(distant))
            def _():
                meet()
                for_neighbours(EARLY, send)

    for end in (0, 1):
        packed[end, BROWS - 1] = pack(BROWS, end)
        packed_rim[end] = pack(edge, end)

    @pl.when(distant)
    def _():
        meet()
        for_neighbours(EARLY, send)

    for_neighbours(LATE, send)

    for_neighbours(SIDES[6:], lambda offset: copies[offset].wait_recv(), -1)
    acc[target] = acc[target] + ra[...]
    for row, side in ((FIRST_BIN, 1), (LAST_BIN, 0)):
        acc[target, row : row + 1, :] = acc[target, row : row + 1, :] + rc[side]
        for b in range(BROWS):
            acc[b + 1, row : row + 1, :] = acc[b + 1, row : row + 1, :] + rb[side, b : b + 1, :]

    for copy in table_copies:
        copy.wait()

    def bins(b, tile):
        lanes = pl.ds(LANES * tile, LANES)
        return [acc[b, 0:SPLIT, lanes], acc[b, STARTS[1] : HELD, lanes]]

    def pair(p, tile):
        return jnp.concatenate(bins(2 * p + 1, tile) + bins(2 * p + 2, tile), axis=0)

    across = lax.broadcasted_iota(jnp.int32, (2 * BCOLS, LANES), 1)

    def resample(p, third, window):
        high, low = parts_of(window)
        result = jnp.dot(
            jnp.concatenate([high, low], axis=1), tab[third], preferred_element_type=jnp.float32
        )
        result = result[:, :LANES] + result[:, LANES:]
        lanes = pl.ds(LANES * third, LANES)
        out[2 * p, :, lanes] = result[:BCOLS]
        out[2 * p + 1, :, lanes] = result[BCOLS:]

    for p in range(BROWS // 2):
        factor = 1.0 / jnp.maximum(pair(p, 2), 1.0)
        low, high = pair(p, 0), pair(p, 1)
        resample(p, 1, jnp.where(across < 64, high, low) * factor)
        resample(p, 0, jnp.where(across < 112, low, 0.0) * factor)
        resample(p, 2, jnp.where(across < 16, 0.0, high) * factor)
        for b in (0, 1):
            for end in (0, 1):
                total = jnp.zeros((8, LANES), jnp.float32)
                for r in range(len(GROUPS)):
                    row = BCOLS * b + 8 * r
                    total = jnp.where(in_group(r, end), factor[row : row + 8], total)
                scale_packed[end, 2 * p + b] = total
    for_neighbours(SIDES, lambda offset: copies[offset].wait_send())

    for_neighbours(SIDES[:6], lambda offset: copies[offset].wait_recv(), -1)

    def halo(end):
        last = len(GROUPS) - 1
        here = in_group(0, end), in_group(last, end)
        near = [jnp.where(here[0], rf[end, 1], 0.0), jnp.where(here[1], pltpu.roll(rf[end, 0], 8 * last, 1), 0.0)]
        far = jnp.where(here[0] & (sublane == 0), rg[end, 1], 0.0)
        turned = pltpu.roll(jnp.broadcast_to(rg[end, 0], (8, LANES)), 8 * last, 1)
        far = far + jnp.where(here[1] & (sublane == 7), turned, 0.0) + re[end]
        rows = []
        for b in range(BROWS):
            tile = rd[end, b]
            tile = tile + jnp.where(sublane == 0, near[0][b : b + 1], 0.0)
            tile = tile + jnp.where(sublane == 7, near[1][b : b + 1], 0.0)
            if b in (0, BROWS - 1):
                tile = tile + jnp.where(target == b + 1, far, 0.0)
            rows.append(tile * scale_packed[end, b])
        high, low = parts_of(jnp.concatenate(rows, axis=0))
        halves = jnp.concatenate([high, low], axis=1)
        result = jnp.dot(halves, tab_ends[end, 0], preferred_element_type=jnp.float32)
        return result + jnp.dot(halves, tab_ends[end, 1], preferred_element_type=jnp.float32)

    before, after = halo(1), halo(0)
    for b in range(BROWS):
        for r in range(len(GROUPS)):
            tile = slice(LANES * (r // 8), LANES * (r // 8 + 1))
            start = 16 * (r % 8)
            rows = pl.ds(8 * r, 8)
            part = before[8 * b : 8 * (b + 1), tile]
            part = pltpu.roll(part, (LANES - start) % LANES, 1) if start else part
            lanes = pl.ds(0, LANES)
            out[b, rows, lanes] = out[b, rows, lanes] + jnp.where(lane < 16, part, 0.0)
            part = after[8 * b : 8 * (b + 1), tile]
            part = pltpu.roll(part, 112 - start, 1) if start < 112 else part
            lanes = pl.ds(2 * LANES, LANES)
            out[b, rows, lanes] = out[b, rows, lanes] + jnp.where(lane >= 112, part, 0.0)


def scoped(n_xl, n_ta, *refs):
    pl.run_scoped(
        lambda load_sem, send_sem: kernel(load_sem, send_sem, n_xl, n_ta, *refs),
        pltpu.SemaphoreType.DMA((5 + len(BLOCKS),)),
        pltpu.SemaphoreType.DMA((len(OFFSETS),)),
    )


def solution(mesh):
    n_xl, n_ta = mesh.shape["xl"], mesh.shape["ta"]
    tables = filter_table(), halo_table()
    f32 = jnp.float32

    def shards(traces, steps):
        return pl.pallas_call(
            functools.partial(scoped, n_xl, n_ta),
            name="stack_resample",
            out_shape=jax.ShapeDtypeStruct((BROWS, BCOLS, OUT), f32),
            in_specs=[pl.BlockSpec(memory_space=pltpu.HBM)] * 4,
            out_specs=pl.BlockSpec(memory_space=pltpu.VMEM),
            scratch_shapes=[
                pltpu.VMEM((ROWS, COLS, SPAN), f32),
                pltpu.VMEM((2, ROWS, 8, SPAN), f32),
                pltpu.VMEM((2, ROWS, COLS), jnp.int32),
                pltpu.VMEM((2, ROWS, SPAN), jnp.int32),
                pltpu.VMEM((3, SPAN, SPAN), jnp.bfloat16),
                pltpu.VMEM((2, 2, SPAN, SPAN), jnp.bfloat16),
                pltpu.VMEM((BROWS, 3 * HALVES[0], SPAN), jnp.bfloat16),
                pltpu.VMEM((BROWS, 3 * HALVES[1], SPAN), jnp.bfloat16),
                pltpu.VMEM((BROWS + 2, HELD, OUT), f32),
                pltpu.VMEM((2, BROWS, 8, LANES), f32),
                pltpu.VMEM((2, 2 * BROWS, OUT), f32),
                pltpu.VMEM((2, BROWS, 8, LANES), f32),
                pltpu.VMEM((2, 8, LANES), f32),
                pltpu.VMEM((HELD, OUT), f32),
                pltpu.VMEM((2, BROWS, OUT), f32),
                pltpu.VMEM((2, 1, OUT), f32),
                pltpu.VMEM((2, BROWS, 8, LANES), f32),
                pltpu.VMEM((2, 8, LANES), f32),
                pltpu.VMEM((2, 2, BROWS, LANES), f32),
                pltpu.VMEM((2, 2, 1, LANES), f32),
                pltpu.SemaphoreType.DMA((len(OFFSETS),)),
            ],
            compiler_params=pltpu.CompilerParams(
                collective_id=0, has_side_effects=True, vmem_limit_bytes=32 * 1024 * 1024
            ),
        )(*(pltpu.with_memory_space_constraint(a, pltpu.HBM) for a in (traces, steps, *map(jnp.asarray, tables))))

    return jax.shard_map(
        shards,
        mesh=mesh,
        in_specs=(P("il", "xl", "ta"), P(None, "il", "xl")),
        out_specs=P("il", "xl", "ta"),
        check_vma=False,
    )
```

time: 11.4 us -> 10.9 us (0.956); the launches traced: 11.3 us -> 10.7 us
  Pallas kernels: 10.2 us -> 9.61 us
    pallas_call x1, Pallas kernels: 10.2 us -> 9.61 us  [shards(): pl.pallas_call(functools.partial(scoped, n_xl, n_ta), name='stack_resampl...]
where the time goes in v4:
time: 10.9 us; the launch traced here: 10.7 us
  Pallas kernels  9.61 us (88%)
  local copies, waits for them, and re-layouts  1.05 us (10%)
    pallas_call x1, Pallas kernels, shards(): pl.pallas_call(functools.partial(scoped, n_xl, n_ta), name='stack_resampl...  9.61 us
    unnamed x1, local copies, waits for them, and re-layouts  1.05 us

profile of v4, /device:TPU:227, one launch (start us, length us, event | category | flops | bytes accessed | tf_op | source)
XLA Modules:
  0.0 10.7 jit_solution(8519960847866100970)
XLA Ops:
  0.0 9.6 %stack_resample.1 = f32[8,104,384]{2,1,0:T(8,128)S(1)} custom-call(f32[16,208,256]{2,1,0:T(8,128)} %refs_0_.1, s32[2,16,208]{2,1,0:T(8,128)} %refs_1_.1, bf16[3,256,256]{2,1,0:T(8,128)(2,1)} %constant.4.clone.refs_2_, bf16[2,2,256,256]{3,2,1,0:T(8,128)(2,1)} %constant.5.clone.refs_3_), custom_call_target="tpu_custom_call" | custom-call | tf_op jit(solution)/shard_map/stack_resample/pallas_call | solution.py:405
  9.6 1.0 %copy.6 = f32[8,104,384]{2,1,0:T(8,128)} copy(f32[8,104,384]{2,1,0:T(8,128)S(1)} %stack_resample.1) | data formatting | bytes 2555904

commit v5 on v4

--- a/solution.py
+++ b/solution.py
@@ -83,7 +83,7 @@
 
 
 def kernel(
-    load_sem, send_sem, n_xl, n_ta, traces, steps, table, ends_table, out,
+    load_sem, send_sem, n_xl, n_ta, traces, steps, table, ends_table, out, fixes,
     x, edges, sv, cbuf, tab, tab_ends, onehot0, onehot1, acc, scale_packed, rims, packed, packed_rim,
     ra, rb, rc, rd, re, rf, rg, recv_sem,
 ):
@@ -372,20 +372,34 @@
         result = jnp.dot(halves, tab_ends[end, 0], preferred_element_type=jnp.float32)
         return result + jnp.dot(halves, tab_ends[end, 1], preferred_element_type=jnp.float32)
 
-    before, after = halo(1), halo(0)
-    for b in range(BROWS):
-        for r in range(len(GROUPS)):
-            tile = slice(LANES * (r // 8), LANES * (r // 8 + 1))
-            start = 16 * (r % 8)
-            rows = pl.ds(8 * r, 8)
-            part = before[8 * b : 8 * (b + 1), tile]
-            part = pltpu.roll(part, (LANES - start) % LANES, 1) if start else part
-            lanes = pl.ds(0, LANES)
-            out[b, rows, lanes] = out[b, rows, lanes] + jnp.where(lane < 16, part, 0.0)
-            part = after[8 * b : 8 * (b + 1), tile]
-            part = pltpu.roll(part, 112 - start, 1) if start < 112 else part
-            lanes = pl.ds(2 * LANES, LANES)
-            out[b, rows, lanes] = out[b, rows, lanes] + jnp.where(lane >= 112, part, 0.0)
+    for end in (0, 1):
+        fixes[end] = halo(end)
+
+
+def finish(sems, own, fixes, out, ends):
+    middle = pl.ds(LANES, LANES)
+    copies = [pltpu.make_async_copy(own.at[:, :, middle], out.at[:, :, middle], sems.at[0])]
+    copies[0].start()
+    lane = lax.broadcasted_iota(jnp.int32, (8, LANES), 1)
+    for p in range(BROWS // 2):
+        for b in (2 * p, 2 * p + 1):
+            for r in range(len(GROUPS)):
+                tile = slice(LANES * (r // 8), LANES * (r // 8 + 1))
+                start = 16 * (r % 8)
+                rows = pl.ds(8 * r, 8)
+                part = fixes[1, 8 * b : 8 * (b + 1), tile]
+                part = pltpu.roll(part, (LANES - start) % LANES, 1) if start else part
+                ends[1, b, rows, :] = own[b, rows, 0:LANES] + jnp.where(lane < 16, part, 0.0)
+                part = fixes[0, 8 * b : 8 * (b + 1), tile]
+                part = pltpu.roll(part, 112 - start, 1) if start < 112 else part
+                ends[0, b, rows, :] = own[b, rows, 2 * LANES : OUT] + jnp.where(lane >= 112, part, 0.0)
+        for end in (0, 1):
+            bs = pl.ds(2 * p, 2)
+            lanes = pl.ds(0 if end else 2 * LANES, LANES)
+            copies.append(pltpu.make_async_copy(ends.at[end, bs], out.at[bs, :, lanes], sems.at[len(copies)]))
+            copies[-1].start()
+    for copy in copies:
+        copy.wait()
 
 
 def scoped(n_xl, n_ta, *refs):
@@ -402,12 +416,15 @@
     f32 = jnp.float32
 
     def shards(traces, steps):
-        return pl.pallas_call(
+        own, fixes = pl.pallas_call(
             functools.partial(scoped, n_xl, n_ta),
             name="stack_resample",
-            out_shape=jax.ShapeDtypeStruct((BROWS, BCOLS, OUT), f32),
+            out_shape=(
+                jax.ShapeDtypeStruct((BROWS, BCOLS, OUT), f32),
+                jax.ShapeDtypeStruct((2, 8 * BROWS, SPAN), f32),
+            ),
             in_specs=[pl.BlockSpec(memory_space=pltpu.HBM)] * 4,
-            out_specs=pl.BlockSpec(memory_space=pltpu.VMEM),
+            out_specs=(pl.BlockSpec(memory_space=pltpu.VMEM),) * 2,
             scratch_shapes=[
                 pltpu.VMEM((ROWS, COLS, SPAN), f32),
                 pltpu.VMEM((2, ROWS, 8, SPAN), f32),
@@ -435,6 +452,19 @@
                 collective_id=0, has_side_effects=True, vmem_limit_bytes=32 * 1024 * 1024
             ),
         )(*(pltpu.with_memory_space_constraint(a, pltpu.HBM) for a in (traces, steps, *map(jnp.asarray, tables))))
+        return pl.pallas_call(
+            lambda *refs: pl.run_scoped(
+                lambda sems: finish(sems, *refs), pltpu.SemaphoreType.DMA((1 + BROWS,))
+            ),
+            name="finish",
+            out_shape=jax.ShapeDtypeStruct((BROWS, BCOLS, OUT), f32),
+            in_specs=[pl.BlockSpec(memory_space=pltpu.VMEM)] * 2,
+            out_specs=pl.BlockSpec(memory_space=pltpu.HBM),
+            scratch_shapes=[
+                pltpu.VMEM((2, BROWS, BCOLS, LANES), f32),
+            ],
+            compiler_params=pltpu.CompilerParams(vmem_limit_bytes=16 * 1024 * 1024),
+        )(own, fixes)
 
     return jax.shard_map(
         shards,

time: 10.9 us -> 10.6 us (0.972)
  local copies, waits for them, and re-layouts: 1.05 us -> 0 us
  Pallas kernels: 9.61 us -> 10.4 us
    unnamed x1 -> x0, local copies, waits for them, and re-layouts: 1.05 us -> none
    pallas_call x0 -> x1, Pallas kernels: none -> 1.03 us  [shards(): pl.pallas_call(lambda *refs: pl.run_scoped(lambda sems: finish(sems, *ref...]
    pallas_call x1, Pallas kernels: 9.61 us -> 9.36 us  [shards(): pl.pallas_call(functools.partial(scoped, n_xl, n_ta), name='stack_resampl...]
where the time goes in v5:
time: 10.6 us; the launch traced here: 10.4 us
  Pallas kernels  10.4 us (98%)
    pallas_call x1, Pallas kernels, shards(): pl.pallas_call(functools.partial(scoped, n_xl, n_ta), name='stack_resampl...  9.36 us
    pallas_call x1, Pallas kernels, shards(): pl.pallas_call(lambda *refs: pl.run_scoped(lambda sems: finish(sems, *ref...  1.03 us

profile of v5, /device:TPU:227, one launch (start us, length us, event | category | flops | bytes accessed | tf_op | source)
XLA Modules:
  0.0 10.4 jit_solution(10775159573338492450)
XLA Ops:
  0.0 9.4 %stack_resample.1 = (f32[8,104,384]{2,1,0:T(8,128)S(1)}, f32[2,64,256]{2,1,0:T(8,128)S(1)}) custom-call(f32[16,208,256]{2,1,0:T(8,128)} %refs_0_.1, s32[2,16,208]{2,1,0:T(8,128)} %refs_1_.1, bf16[3,256,256]{2,1,0:T(8,128)(2,1)} %constant.4.clone.refs_2_, bf16[2,2,256,256]{3,2,1,0:T(8,128)(2,1)} %constant.5.clone.refs_3_), custom_call_target="tpu_custom_call" | custom-call | tf_op jit(solution)/shard_map/stack_resample/pallas_call | solution.py:419
  9.4 1.0 %finish.1 = f32[8,104,384]{2,1,0:T(8,128)} custom-call(f32[8,104,384]{2,1,0:T(8,128)S(1)} %get-tuple-element.7.refs_0_, f32[2,64,256]{2,1,0:T(8,128)S(1)} %get-tuple-element.8.refs_1_), custom_call_target="tpu_custom_call" | custom-call | tf_op jit(solution)/shard_map/finish/pallas_call | solution.py:455

commit v6 on v5

--- a/solution.py
+++ b/solution.py
@@ -32,7 +32,7 @@
 SIDES = ((-1, -1), (-1, 1), (1, -1), (1, 1), (0, -1), (0, 1), (-1, 0), (1, 0), (0, 0))
 EARLY = SIDES[:4] + SIDES[6:8]
 LATE = SIDES[4:6] + SIDES[8:]
-BLOCKS = (range(0, 4), range(4, 8))
+BLOCKS = (range(0, 3), range(3, 8))
 
 
 def filter_table():
@@ -71,6 +71,12 @@
     )
 
 
+def in_group(r, end):
+    start = (8 * r + (120 if end else 0)) % LANES
+    lane = lax.broadcasted_iota(jnp.int32, (8, LANES), 1)
+    return (lane >= start) & (lane < start + 8)
+
+
 def parts_of(values):
     high = values.astype(jnp.bfloat16)
     low = (values - high.astype(jnp.float32)).astype(jnp.bfloat16)
@@ -83,9 +89,9 @@
 
 
 def kernel(
-    load_sem, send_sem, n_xl, n_ta, traces, steps, table, ends_table, out, fixes,
-    x, edges, sv, cbuf, tab, tab_ends, onehot0, onehot1, acc, scale_packed, rims, packed, packed_rim,
-    ra, rb, rc, rd, re, rf, rg, recv_sem,
+    load_sem, send_sem, n_xl, n_ta, traces, steps, table, ends_table, out, tab_ends, scale_packed, rd, re, rf, rg,
+    x, edges, sv, cbuf, tab, onehot0, onehot1, acc, rims, packed, packed_rim,
+    ra, rb, rc, recv_sem,
 ):
     il, xl, ta = lax.axis_index("il"), lax.axis_index("xl"), lax.axis_index("ta")
 
@@ -223,12 +229,6 @@
             )
 
     lane = lax.broadcasted_iota(jnp.int32, (8, LANES), 1)
-    sublane = lax.broadcasted_iota(jnp.int32, (8, LANES), 0)
-
-    def in_group(r, end):
-        start = (8 * r + (120 if end else 0)) % LANES
-        return (lane >= start) & (lane < start + 8)
-
     def pack(b, end):
         tile = pl.ds(LANES * end, LANES)
         total = acc[b, 0:8, tile]
@@ -352,6 +352,15 @@
 
     for_neighbours(SIDES[:6], lambda offset: copies[offset].wait_recv(), -1)
 
+
+def finish(sems, own, tab_ends, scale_packed, rd, re, rf, rg, out, ends):
+    middle = pl.ds(LANES, LANES)
+    copies = [pltpu.make_async_copy(own.at[:, :, middle], out.at[:, :, middle], sems.at[0])]
+    copies[0].start()
+    lane = lax.broadcasted_iota(jnp.int32, (8, LANES), 1)
+    sublane = lax.broadcasted_iota(jnp.int32, (8, LANES), 0)
+    target = BROWS - (BROWS - 1) * lax.axis_index("il")
+
     def halo(end):
         last = len(GROUPS) - 1
         here = in_group(0, end), in_group(last, end)
@@ -372,25 +381,17 @@
         result = jnp.dot(halves, tab_ends[end, 0], preferred_element_type=jnp.float32)
         return result + jnp.dot(halves, tab_ends[end, 1], preferred_element_type=jnp.float32)
 
-    for end in (0, 1):
-        fixes[end] = halo(end)
-
-
-def finish(sems, own, fixes, out, ends):
-    middle = pl.ds(LANES, LANES)
-    copies = [pltpu.make_async_copy(own.at[:, :, middle], out.at[:, :, middle], sems.at[0])]
-    copies[0].start()
-    lane = lax.broadcasted_iota(jnp.int32, (8, LANES), 1)
+    fixes = halo(0), halo(1)
     for p in range(BROWS // 2):
         for b in (2 * p, 2 * p + 1):
             for r in range(len(GROUPS)):
                 tile = slice(LANES * (r // 8), LANES * (r // 8 + 1))
                 start = 16 * (r % 8)
                 rows = pl.ds(8 * r, 8)
-                part = fixes[1, 8 * b : 8 * (b + 1), tile]
+                part = fixes[1][8 * b : 8 * (b + 1), tile]
                 part = pltpu.roll(part, (LANES - start) % LANES, 1) if start else part
                 ends[1, b, rows, :] = own[b, rows, 0:LANES] + jnp.where(lane < 16, part, 0.0)
-                part = fixes[0, 8 * b : 8 * (b + 1), tile]
+                part = fixes[0][8 * b : 8 * (b + 1), tile]
                 part = pltpu.roll(part, 112 - start, 1) if start < 112 else part
                 ends[0, b, rows, :] = own[b, rows, 2 * LANES : OUT] + jnp.where(lane >= 112, part, 0.0)
         for end in (0, 1):
@@ -416,36 +417,35 @@
     f32 = jnp.float32
 
     def shards(traces, steps):
-        own, fixes = pl.pallas_call(
+        found = pl.pallas_call(
             functools.partial(scoped, n_xl, n_ta),
             name="stack_resample",
             out_shape=(
                 jax.ShapeDtypeStruct((BROWS, BCOLS, OUT), f32),
-                jax.ShapeDtypeStruct((2, 8 * BROWS, SPAN), f32),
+                jax.ShapeDtypeStruct((2, 2, SPAN, SPAN), jnp.bfloat16),
+                jax.ShapeDtypeStruct((2, BROWS, 8, LANES), f32),
+                jax.ShapeDtypeStruct((2, BROWS, 8, LANES), f32),
+                jax.ShapeDtypeStruct((2, 8, LANES), f32),
+                jax.ShapeDtypeStruct((2, 2, BROWS, LANES), f32),
+                jax.ShapeDtypeStruct((2, 2, 1, LANES), f32),
             ),
             in_specs=[pl.BlockSpec(memory_space=pltpu.HBM)] * 4,
-            out_specs=(pl.BlockSpec(memory_space=pltpu.VMEM),) * 2,
+            out_specs=(pl.BlockSpec(memory_space=pltpu.VMEM),) * 7,
             scratch_shapes=[
                 pltpu.VMEM((ROWS, COLS, SPAN), f32),
                 pltpu.VMEM((2, ROWS, 8, SPAN), f32),
                 pltpu.VMEM((2, ROWS, COLS), jnp.int32),
                 pltpu.VMEM((2, ROWS, SPAN), jnp.int32),
                 pltpu.VMEM((3, SPAN, SPAN), jnp.bfloat16),
-                pltpu.VMEM((2, 2, SPAN, SPAN), jnp.bfloat16),
                 pltpu.VMEM((BROWS, 3 * HALVES[0], SPAN), jnp.bfloat16),
                 pltpu.VMEM((BROWS, 3 * HALVES[1], SPAN), jnp.bfloat16),
                 pltpu.VMEM((BROWS + 2, HELD, OUT), f32),
-                pltpu.VMEM((2, BROWS, 8, LANES), f32),
                 pltpu.VMEM((2, 2 * BROWS, OUT), f32),
                 pltpu.VMEM((2, BROWS, 8, LANES), f32),
                 pltpu.VMEM((2, 8, LANES), f32),
                 pltpu.VMEM((HELD, OUT), f32),
                 pltpu.VMEM((2, BROWS, OUT), f32),
                 pltpu.VMEM((2, 1, OUT), f32),
-                pltpu.VMEM((2, BROWS, 8, LANES), f32),
-                pltpu.VMEM((2, 8, LANES), f32),
-                pltpu.VMEM((2, 2, BROWS, LANES), f32),
-                pltpu.VMEM((2, 2, 1, LANES), f32),
                 pltpu.SemaphoreType.DMA((len(OFFSETS),)),
             ],
             compiler_params=pltpu.CompilerParams(
@@ -458,13 +458,13 @@
             ),
             name="finish",
             out_shape=jax.ShapeDtypeStruct((BROWS, BCOLS, OUT), f32),
-            in_specs=[pl.BlockSpec(memory_space=pltpu.VMEM)] * 2,
+            in_specs=[pl.BlockSpec(memory_space=pltpu.VMEM)] * 7,
             out_specs=pl.BlockSpec(memory_space=pltpu.HBM),
             scratch_shapes=[
                 pltpu.VMEM((2, BROWS, BCOLS, LANES), f32),
             ],
             compiler_params=pltpu.CompilerParams(vmem_limit_bytes=16 * 1024 * 1024),
-        )(own, fixes)
+        )(*found)
 
     return jax.shard_map(
         shards,

time: 10.6 us -> 10.6 us (level)
  the two profiles are of different devices: /device:TPU:227 before, /device:TPU:121 now
where the time goes in v6:
time: 10.6 us; the launch traced here: 10.5 us
  Pallas kernels  10.5 us (99%)
    pallas_call x1, Pallas kernels, shards(): pl.pallas_call(functools.partial(scoped, n_xl, n_ta), name='stack_resampl...  9.22 us
    pallas_call x1, Pallas kernels, shards(): pl.pallas_call(lambda *refs: pl.run_scoped(lambda sems: finish(sems, *ref...  1.25 us

profile of v6, /device:TPU:121, one launch (start us, length us, event | category | flops | bytes accessed | tf_op | source)
XLA Modules:
  0.0 10.5 jit_solution(2718873650845122602)
XLA Ops:
  0.0 9.2 %stack_resample.1 = (f32[8,104,384]{2,1,0:T(8,128)S(1)}, bf16[2,2,256,256]{3,2,1,0:T(8,128)(2,1)S(1)}, f32[2,8,8,128]{3,2,1,0:T(8,128)S(1)}, f32[2,8,8,128]{3,2,...) custom-call(f32[16,208,256]{2,1,0:T(8,128)} %refs_0_.1, ...), custom_call_target="tpu_custom_call" | custom-call | tf_op jit(solution)/shard_map/stack_resample/pallas_call | solution.py:420
  9.2 1.2 %finish.1 = f32[8,104,384]{2,1,0:T(8,128)} custom-call(f32[8,104,384]{2,1,0:T(8,128)S(1)} %get-tuple-element.12.refs_0_, bf16[2,2,256,256]{3,2,1,0:T(8,128)(2,1)S(1)} %get-tuple-element.13.refs_1_, f32[2,8,8,128]{3,2,1,0:T(8,128)S(1)} %get-tuple-element.14.refs_2_, f32[2,8,8,128]{3,2,1,0:T(8,128)S(1)} %get-tuple-element.15.refs_3_, ...), custom_call_target="tpu_custom_call" | custom-call | tf_op jit(solution)/shard_map/finish/pallas_call | solution.py:455

commit v7 on v6

--- a/solution.py
+++ b/solution.py
@@ -89,9 +89,9 @@
 
 
 def kernel(
-    load_sem, send_sem, n_xl, n_ta, traces, steps, table, ends_table, out, tab_ends, scale_packed, rd, re, rf, rg,
+    load_sem, send_sem, n_xl, n_ta, traces, steps, table, ends_table, out, tab_ends, scale_packed, fixes, rf, rg,
     x, edges, sv, cbuf, tab, onehot0, onehot1, acc, rims, packed, packed_rim,
-    ra, rb, rc, recv_sem,
+    ra, rb, rc, rd, re, recv_sem,
 ):
     il, xl, ta = lax.axis_index("il"), lax.axis_index("xl"), lax.axis_index("ta")
 
@@ -350,10 +350,26 @@
                 scale_packed[end, 2 * p + b] = total
     for_neighbours(SIDES, lambda offset: copies[offset].wait_send())
 
-    for_neighbours(SIDES[:6], lambda offset: copies[offset].wait_recv(), -1)
-
-
-def finish(sems, own, tab_ends, scale_packed, rd, re, rf, rg, out, ends):
+    for_neighbours(SIDES[4:6], lambda offset: copies[offset].wait_recv(), -1)
+    for end in (0, 1):
+        rows = []
+        for b in range(BROWS):
+            tile = rd[end, b]
+            if b in (0, BROWS - 1):
+                tile = tile + jnp.where(target == b + 1, re[end], 0.0)
+            rows.append(tile * scale_packed[end, b])
+        fixes[end] = halo_product(jnp.concatenate(rows, axis=0), tab_ends, end)
+    for_neighbours(SIDES[:4], lambda offset: copies[offset].wait_recv(), -1)
+
+
+def halo_product(packed, tab_ends, end):
+    high, low = parts_of(packed)
+    halves = jnp.concatenate([high, low], axis=1)
+    result = jnp.dot(halves, tab_ends[end, 0], preferred_element_type=jnp.float32)
+    return result + jnp.dot(halves, tab_ends[end, 1], preferred_element_type=jnp.float32)
+
+
+def finish(sems, own, tab_ends, scale_packed, fixes, rf, rg, out, ends):
     middle = pl.ds(LANES, LANES)
     copies = [pltpu.make_async_copy(own.at[:, :, middle], out.at[:, :, middle], sems.at[0])]
     copies[0].start()
@@ -361,39 +377,36 @@
     sublane = lax.broadcasted_iota(jnp.int32, (8, LANES), 0)
     target = BROWS - (BROWS - 1) * lax.axis_index("il")
 
-    def halo(end):
-        last = len(GROUPS) - 1
-        here = in_group(0, end), in_group(last, end)
-        near = [jnp.where(here[0], rf[end, 1], 0.0), jnp.where(here[1], pltpu.roll(rf[end, 0], 8 * last, 1), 0.0)]
-        far = jnp.where(here[0] & (sublane == 0), rg[end, 1], 0.0)
-        turned = pltpu.roll(jnp.broadcast_to(rg[end, 0], (8, LANES)), 8 * last, 1)
-        far = far + jnp.where(here[1] & (sublane == 7), turned, 0.0) + re[end]
+    last = len(GROUPS) - 1
+
+    def rims(end):
         rows = []
-        for b in range(BROWS):
-            tile = rd[end, b]
-            tile = tile + jnp.where(sublane == 0, near[0][b : b + 1], 0.0)
-            tile = tile + jnp.where(sublane == 7, near[1][b : b + 1], 0.0)
-            if b in (0, BROWS - 1):
-                tile = tile + jnp.where(target == b + 1, far, 0.0)
-            rows.append(tile * scale_packed[end, b])
-        high, low = parts_of(jnp.concatenate(rows, axis=0))
-        halves = jnp.concatenate([high, low], axis=1)
-        result = jnp.dot(halves, tab_ends[end, 0], preferred_element_type=jnp.float32)
-        return result + jnp.dot(halves, tab_ends[end, 1], preferred_element_type=jnp.float32)
-
-    fixes = halo(0), halo(1)
+        for r, side, line in ((0, 1, 0), (last, 0, 7)):
+            near, far = rf[end, side], jnp.broadcast_to(rg[end, side], (8, LANES))
+            both = near + jnp.where(sublane == target - 1, far, 0.0)
+            both = pltpu.roll(both, 8 * r, 1) if r else both
+            rows.append(jnp.where(in_group(r, end), both, 0.0) * scale_packed[end, :, line, :])
+        result = halo_product(jnp.concatenate(rows, axis=0), tab_ends, end)
+        return result[:8, :LANES], result[8:, LANES:]
+
+    added = rims(0), rims(1)
+
+    def part_of(b, r, end):
+        tile = slice(LANES * (r // 8), LANES * (r // 8 + 1))
+        part = fixes[end, 8 * b : 8 * (b + 1), tile]
+        if r in (0, last):
+            here = sublane == (0 if r == 0 else 7)
+            part = part + jnp.where(here, added[end][0 if r == 0 else 1][b : b + 1], 0.0)
+        turn = ((0 if end else 112) - 16 * (r % 8)) % LANES
+        part = pltpu.roll(part, turn, 1) if turn else part
+        return jnp.where(lane < 16 if end else lane >= 112, part, 0.0)
+
     for p in range(BROWS // 2):
         for b in (2 * p, 2 * p + 1):
             for r in range(len(GROUPS)):
-                tile = slice(LANES * (r // 8), LANES * (r // 8 + 1))
-                start = 16 * (r % 8)
                 rows = pl.ds(8 * r, 8)
-                part = fixes[1][8 * b : 8 * (b + 1), tile]
-                part = pltpu.roll(part, (LANES - start) % LANES, 1) if start else part
-                ends[1, b, rows, :] = own[b, rows, 0:LANES] + jnp.where(lane < 16, part, 0.0)
-                part = fixes[0][8 * b : 8 * (b + 1), tile]
-                part = pltpu.roll(part, 112 - start, 1) if start < 112 else part
-                ends[0, b, rows, :] = own[b, rows, 2 * LANES : OUT] + jnp.where(lane >= 112, part, 0.0)
+                ends[1, b, rows, :] = own[b, rows, 0:LANES] + part_of(b, r, 1)
+                ends[0, b, rows, :] = own[b, rows, 2 * LANES : OUT] + part_of(b, r, 0)
         for end in (0, 1):
             bs = pl.ds(2 * p, 2)
             lanes = pl.ds(0 if end else 2 * LANES, LANES)
@@ -424,13 +437,12 @@
                 jax.ShapeDtypeStruct((BROWS, BCOLS, OUT), f32),
                 jax.ShapeDtypeStruct((2, 2, SPAN, SPAN), jnp.bfloat16),
                 jax.ShapeDtypeStruct((2, BROWS, 8, LANES), f32),
-                jax.ShapeDtypeStruct((2, BROWS, 8, LANES), f32),
-                jax.ShapeDtypeStruct((2, 8, LANES), f32),
+                jax.ShapeDtypeStruct((2, 8 * BROWS, SPAN), f32),
                 jax.ShapeDtypeStruct((2, 2, BROWS, LANES), f32),
                 jax.ShapeDtypeStruct((2, 2, 1, LANES), f32),
             ),
             in_specs=[pl.BlockSpec(memory_space=pltpu.HBM)] * 4,
-            out_specs=(pl.BlockSpec(memory_space=pltpu.VMEM),) * 7,
+            out_specs=(pl.BlockSpec(memory_space=pltpu.VMEM),) * 6,
             scratch_shapes=[
                 pltpu.VMEM((ROWS, COLS, SPAN), f32),
                 pltpu.VMEM((2, ROWS, 8, SPAN), f32),
@@ -446,6 +458,8 @@
                 pltpu.VMEM((HELD, OUT), f32),
                 pltpu.VMEM((2, BROWS, OUT), f32),
                 pltpu.VMEM((2, 1, OUT), f32),
+                pltpu.VMEM((2, BROWS, 8, LANES), f32),
+                pltpu.VMEM((2, 8, LANES), f32),
                 pltpu.SemaphoreType.DMA((len(OFFSETS),)),
             ],
             compiler_params=pltpu.CompilerParams(
@@ -458,7 +472,7 @@
             ),
             name="finish",
             out_shape=jax.ShapeDtypeStruct((BROWS, BCOLS, OUT), f32),
-            in_specs=[pl.BlockSpec(memory_space=pltpu.VMEM)] * 7,
+            in_specs=[pl.BlockSpec(memory_space=pltpu.VMEM)] * 6,
             out_specs=pl.BlockSpec(memory_space=pltpu.HBM),
             scratch_shapes=[
                 pltpu.VMEM((2, BROWS, BCOLS, LANES), f32),

time: 10.6 us -> 10.6 us (level)
  the two profiles are of different devices: /device:TPU:121 before, /device:TPU:227 now
where the time goes in v7:
time: 10.6 us; the launch traced here: 10.4 us
  Pallas kernels  10.4 us (98%)
    pallas_call x1, Pallas kernels, shards(): pl.pallas_call(functools.partial(scoped, n_xl, n_ta), name='stack_resampl...  9.14 us
    pallas_call x1, Pallas kernels, shards(): pl.pallas_call(lambda *refs: pl.run_scoped(lambda sems: finish(sems, *ref...  1.28 us

profile of v7, /device:TPU:227, one launch (start us, length us, event | category | flops | bytes accessed | tf_op | source)
XLA Modules:
  0.0 10.4 jit_solution(4722506860714777668)
XLA Ops:
  0.0 9.1 %stack_resample.1 = (f32[8,104,384]{2,1,0:T(8,128)S(1)}, bf16[2,2,256,256]{3,2,1,0:T(8,128)(2,1)S(1)}, f32[2,8,8,128]{3,2,1,0:T(8,128)S(1)}, f32[2,64,256]{2,1,0...) custom-call(f32[16,208,256]{2,1,0:T(8,128)} %refs_0_.1, s32[2,16,208]{2,1,0:T(8,128)} %refs_1_.1, ...), custom_call_target="tpu_custom_call" | custom-call | tf_op jit(solution)/shard_map/stack_resample/pallas_call | solution.py:433
  9.1 1.3 %finish.1 = f32[8,104,384]{2,1,0:T(8,128)} custom-call(f32[8,104,384]{2,1,0:T(8,128)S(1)} %get-tuple-element.11.refs_0_, bf16[2,2,256,256]{3,2,1,0:T(8,128)(2,1)S(1)} %get-tuple-element.12.refs_1_, f32[2,8,8,128]{3,2,1,0:T(8,128)S(1)} %get-tuple-element.13.refs_2_, f32[2,64,256]{2,1,0:T(8,128)S(1)} %get-tuple-element.14.refs_3_, ...), custom_call_target="tpu_custom_call" | custom-call | tf_op jit(solution)/shard_map/finish/pallas_call | solution.py:469

commit v8 on v7

--- a/solution.py
+++ b/solution.py
@@ -71,6 +71,18 @@
     )
 
 
+def rim_table():
+    weights = np.zeros((2, LANES, LANES), np.float32)
+    sample = np.arange(8)[:, None]
+    for end in (0, 1):
+        n = sample - 8 if end else sample + SPAN
+        x = (Q * (np.arange(16)[None, :] + (0 if end else OUT - 16)) - P_SIZE * n) / P_SIZE
+        part = np.where(np.abs(x) < REACH, np.sinc(x) * np.sinc(x / REACH), 0.0)
+        first, place = (LANES - 8, 0) if end else (0, LANES - 16)
+        weights[end, first : first + 8, place : place + 16] = part
+    return weights
+
+
 def in_group(r, end):
     start = (8 * r + (120 if end else 0)) % LANES
     lane = lax.broadcasted_iota(jnp.int32, (8, LANES), 1)
@@ -89,8 +101,8 @@
 
 
 def kernel(
-    load_sem, send_sem, n_xl, n_ta, traces, steps, table, ends_table, out, tab_ends, scale_packed, fixes, rf, rg,
-    x, edges, sv, cbuf, tab, onehot0, onehot1, acc, rims, packed, packed_rim,
+    load_sem, send_sem, n_xl, n_ta, traces, steps, table, ends_table, rims_table, out, rim_scale, fixes, rf, rg,
+    x, edges, sv, cbuf, tab, tab_ends, tab_rims, onehot0, onehot1, acc, scale_packed, rims, reach, packed, packed_rim,
     ra, rb, rc, rd, re, recv_sem,
 ):
     il, xl, ta = lax.axis_index("il"), lax.axis_index("xl"), lax.axis_index("ta")
@@ -131,6 +143,8 @@
         columns = pl.ds((COLS - 8) * side, 8)
         edge_copies.append(pltpu.make_async_copy(traces.at[:, columns, :], edges.at[side], load_sem.at[1 + side]))
         edge_copies[-1].start()
+    edge_copies.append(pltpu.make_async_copy(rims_table, tab_rims, load_sem.at[5 + len(BLOCKS)]))
+    edge_copies[-1].start()
     loads = []
     for block in BLOCKS:
         rows = pl.ds(2 * block[0], 2 * len(block))
@@ -151,7 +165,6 @@
     for number, offset in enumerate(OFFSETS):
         di, dx, dt = offset
         side, end = (dx + 1) // 2, (dt + 1) // 2
-        lanes = pl.ds(LANES * end, LANES)
         if dt == 0 and dx == 0:
             source, place = acc.at[edge], ra
         elif dt == 0:
@@ -159,9 +172,9 @@
         elif dx == 0:
             source, place = (packed_rim.at[end], re.at[end]) if di else (packed.at[end], rd.at[end])
         elif di:
-            source, place = rims.at[side, far, lanes], rg.at[end, side]
+            source, place = reach.at[end, side, far], rg.at[end, side]
         else:
-            source, place = rims.at[side, own, lanes], rf.at[end, side]
+            source, place = reach.at[end, side, own], rf.at[end, side]
         copies[offset] = pltpu.make_async_remote_copy(
             src_ref=source,
             dst_ref=place,
@@ -187,59 +200,11 @@
             for place in (rd.at[end], re.at[end], rf.at[end], rg.at[end]):
                 place[...] = jnp.zeros(place.shape, jnp.float32)
 
-    steps_copy.wait()
+    for copy in (steps_copy, *edge_copies):
+        copy.wait()
     row_bin = lax.shift_right_logical(lax.broadcasted_iota(jnp.int32, (ROWS, COLS), 0), 1) + sv[0]
     inside = (row_bin >= 0) & (row_bin < BROWS)
     row_code = jnp.where(inside, row_bin, jnp.where(row_bin == edge - 1, BROWS, -1))
-    wide = lax.broadcasted_iota(jnp.int32, (ROWS, SPAN), 1)
-    bin_col = lax.shift_right_logical(lax.broadcasted_iota(jnp.int32, (ROWS, COLS), 1), 1) + sv[1]
-    cbuf[...] = jnp.full(cbuf.shape, -1, jnp.int32)
-    cbuf[0, :, 0:COLS] = jnp.where(
-        (bin_col >= 0) & (bin_col < SPLIT), (sv[0] + 1) * HALVES[0] + bin_col, -1
-    )
-    cbuf[1, :, 0:COLS] = jnp.where(
-        (bin_col >= SPLIT) & (bin_col < BCOLS), (sv[0] + 1) * HALVES[1] + bin_col - SPLIT, -1
-    )
-    first, second = cbuf[0], cbuf[1]
-    codes = (
-        (
-            jnp.where(wide < 120, first, -1),
-            jnp.where((wide >= 120) & (wide < 240), pltpu.roll(first, 120, 1), -1),
-        ),
-        (
-            jnp.where(wide < 104, pltpu.roll(second, SPAN - 104, 1), -1),
-            jnp.where((wide >= 104) & (wide < 208), second, -1),
-        ),
-    )
-    onehot = (onehot0, onehot1)
-    for h, size in enumerate(HALVES):
-        places = lax.broadcasted_iota(jnp.int32, (3 * size, SPAN), 0)
-        even, odd = codes[h]
-        for k in range(BROWS):
-            code = jnp.maximum(even[2 * k : 2 * k + 1], odd[2 * k + 1 : 2 * k + 2])
-            onehot[h][k] = jnp.where(places == code, 1.0, 0.0).astype(jnp.bfloat16)
-
-    for b in range(BROWS + 2):
-        for h, size in enumerate(HALVES):
-            rows = [onehot[h][k, size * (b - k) : size * (b - k + 1), :] for k in range(BROWS) if 0 <= b - k < 3]
-            total = functools.reduce(jnp.add, rows)
-            total = (total[:, :LANES] + total[:, LANES:]).astype(jnp.float32)
-            acc[b, STARTS[h] : STARTS[h] + size, SPAN:OUT] = jnp.broadcast_to(
-                jnp.sum(total, axis=1, keepdims=True), (size, LANES)
-            )
-
-    lane = lax.broadcasted_iota(jnp.int32, (8, LANES), 1)
-    def pack(b, end):
-        tile = pl.ds(LANES * end, LANES)
-        total = acc[b, 0:8, tile]
-        for r in range(1, len(GROUPS)):
-            turned = pltpu.roll(acc[b, GROUPS[r] : GROUPS[r] + 8, tile], 8 * r, 1)
-            total = jnp.where(in_group(r, end), turned, total)
-        return total
-
-    def send(offset):
-        copies[offset].start()
-
     def find_rims():
         slots = lax.broadcasted_iota(jnp.int32, (ROWS, 2 * BROWS), 1)
         ones = jnp.ones((2 * ROWS, LANES), jnp.float32)
@@ -257,6 +222,67 @@
                 precision=lax.Precision.HIGHEST,
                 preferred_element_type=jnp.float32,
             )
+        for end in (0, 1):
+            tiles = [rims[side, :, LANES * end : LANES * (end + 1)] for side in (0, 1)]
+            product = jnp.dot(
+                jnp.concatenate(tiles, axis=0),
+                tab_rims[end],
+                precision=lax.Precision.HIGHEST,
+                preferred_element_type=jnp.float32,
+            )
+            for side in (0, 1):
+                reach[end, side] = product[2 * BROWS * side : 2 * BROWS * (side + 1)]
+
+    find_rims()
+
+    wide = lax.broadcasted_iota(jnp.int32, (ROWS, SPAN), 1)
+    bin_col = lax.shift_right_logical(lax.broadcasted_iota(jnp.int32, (ROWS, COLS), 1), 1) + sv[1]
+    cbuf[...] = jnp.full(cbuf.shape, -1, jnp.int32)
+    cbuf[0, :, 0:COLS] = jnp.where(
+        (bin_col >= 0) & (bin_col < SPLIT), (sv[0] + 1) * HALVES[0] + bin_col, -1
+    )
+    cbuf[1, :, 0:COLS] = jnp.where(
+        (bin_col >= SPLIT) & (bin_col < BCOLS), (sv[0] + 1) * HALVES[1] + bin_col - SPLIT, -1
+    )
+    first, second = cbuf[0], cbuf[1]
+    codes = (
+        (
+            jnp.where(wide < 120, first, -1),
+            jnp.where((wide >= 120) & (wide < 240), pltpu.roll(first, 120, 1), -1),
+        ),
+        (
+            jnp.where(wide < 104, pltpu.roll(second, SPAN - 104, 1), -1),
+            jnp.where((wide >= 104) & (wide < 208), second, -1),
+        ),
+    )
+    onehot = (onehot0, onehot1)
+    for h, size in enumerate(HALVES):
+        places = lax.broadcasted_iota(jnp.int32, (3 * size, SPAN), 0)
+        even, odd = codes[h]
+        for k in range(BROWS):
+            code = jnp.maximum(even[2 * k : 2 * k + 1], odd[2 * k + 1 : 2 * k + 2])
+            onehot[h][k] = jnp.where(places == code, 1.0, 0.0).astype(jnp.bfloat16)
+
+    for b in range(BROWS + 2):
+        for h, size in enumerate(HALVES):
+            rows = [onehot[h][k, size * (b - k) : size * (b - k + 1), :] for k in range(BROWS) if 0 <= b - k < 3]
+            total = functools.reduce(jnp.add, rows)
+            total = (total[:, :LANES] + total[:, LANES:]).astype(jnp.float32)
+            acc[b, STARTS[h] : STARTS[h] + size, SPAN:OUT] = jnp.broadcast_to(
+                jnp.sum(total, axis=1, keepdims=True), (size, LANES)
+            )
+
+    lane = lax.broadcasted_iota(jnp.int32, (8, LANES), 1)
+    def pack(b, end):
+        tile = pl.ds(LANES * end, LANES)
+        total = acc[b, 0:8, tile]
+        for r in range(1, len(GROUPS)):
+            turned = pltpu.roll(acc[b, GROUPS[r] : GROUPS[r] + 8, tile], 8 * r, 1)
+            total = jnp.where(in_group(r, end), turned, total)
+        return total
+
+    def send(offset):
+        copies[offset].start()
 
     distant = (lax.rem(ta, 4) == 0) | (ta == n_ta // 2 - 1)
 
@@ -267,10 +293,6 @@
 
     for block, load in zip(BLOCKS, loads):
         load.wait()
-        if block is BLOCKS[0]:
-            for copy in edge_copies:
-                copy.wait()
-            find_rims()
         for k in block:
             for h, size in enumerate(HALVES):
                 start, stop = WINDOWS[h]
@@ -342,6 +364,9 @@
         resample(p, 0, jnp.where(across < 112, low, 0.0) * factor)
         resample(p, 2, jnp.where(across < 16, 0.0, high) * factor)
         for b in (0, 1):
+            for n, c in enumerate((0, BCOLS - 1)):
+                row = BCOLS * b + c
+                rim_scale[n, 2 * p + b : 2 * p + b + 1, :] = factor[row : row + 1]
             for end in (0, 1):
                 total = jnp.zeros((8, LANES), jnp.float32)
                 for r in range(len(GROUPS)):
@@ -369,7 +394,7 @@
     return result + jnp.dot(halves, tab_ends[end, 1], preferred_element_type=jnp.float32)
 
 
-def finish(sems, own, tab_ends, scale_packed, fixes, rf, rg, out, ends):
+def finish(sems, own, rim_scale, fixes, rf, rg, out, ends):
     middle = pl.ds(LANES, LANES)
     copies = [pltpu.make_async_copy(own.at[:, :, middle], out.at[:, :, middle], sems.at[0])]
     copies[0].start()
@@ -379,27 +404,22 @@
 
     last = len(GROUPS) - 1
 
-    def rims(end):
-        rows = []
-        for r, side, line in ((0, 1, 0), (last, 0, 7)):
-            near, far = rf[end, side], jnp.broadcast_to(rg[end, side], (8, LANES))
-            both = near + jnp.where(sublane == target - 1, far, 0.0)
-            both = pltpu.roll(both, 8 * r, 1) if r else both
-            rows.append(jnp.where(in_group(r, end), both, 0.0) * scale_packed[end, :, line, :])
-        result = halo_product(jnp.concatenate(rows, axis=0), tab_ends, end)
-        return result[:8, :LANES], result[8:, LANES:]
-
-    added = rims(0), rims(1)
+    def rims(end, n):
+        far = jnp.where(sublane == target - 1, jnp.broadcast_to(rg[end, 1 - n], (8, LANES)), 0.0)
+        return (rf[end, 1 - n] + far) * rim_scale[n]
+
+    added = [[rims(end, n) for n in (0, 1)] for end in (0, 1)]
 
     def part_of(b, r, end):
         tile = slice(LANES * (r // 8), LANES * (r // 8 + 1))
         part = fixes[end, 8 * b : 8 * (b + 1), tile]
-        if r in (0, last):
-            here = sublane == (0 if r == 0 else 7)
-            part = part + jnp.where(here, added[end][0 if r == 0 else 1][b : b + 1], 0.0)
         turn = ((0 if end else 112) - 16 * (r % 8)) % LANES
         part = pltpu.roll(part, turn, 1) if turn else part
-        return jnp.where(lane < 16 if end else lane >= 112, part, 0.0)
+        part = jnp.where(lane < 16 if end else lane >= 112, part, 0.0)
+        if r in (0, last):
+            n = min(r, 1)
+            part = part + jnp.where(sublane == 7 * n, added[end][n][b : b + 1], 0.0)
+        return part
 
     for p in range(BROWS // 2):
         for b in (2 * p, 2 * p + 1):
@@ -419,14 +439,14 @@
 def scoped(n_xl, n_ta, *refs):
     pl.run_scoped(
         lambda load_sem, send_sem: kernel(load_sem, send_sem, n_xl, n_ta, *refs),
-        pltpu.SemaphoreType.DMA((5 + len(BLOCKS),)),
+        pltpu.SemaphoreType.DMA((6 + len(BLOCKS),)),
         pltpu.SemaphoreType.DMA((len(OFFSETS),)),
     )
 
 
 def solution(mesh):
     n_xl, n_ta = mesh.shape["xl"], mesh.shape["ta"]
-    tables = filter_table(), halo_table()
+    tables = filter_table(), halo_table(), rim_table()
     f32 = jnp.float32
 
     def shards(traces, steps):
@@ -435,24 +455,27 @@
             name="stack_resample",
             out_shape=(
                 jax.ShapeDtypeStruct((BROWS, BCOLS, OUT), f32),
-                jax.ShapeDtypeStruct((2, 2, SPAN, SPAN), jnp.bfloat16),
-                jax.ShapeDtypeStruct((2, BROWS, 8, LANES), f32),
+                jax.ShapeDtypeStruct((2, BROWS, LANES), f32),
                 jax.ShapeDtypeStruct((2, 8 * BROWS, SPAN), f32),
                 jax.ShapeDtypeStruct((2, 2, BROWS, LANES), f32),
                 jax.ShapeDtypeStruct((2, 2, 1, LANES), f32),
             ),
-            in_specs=[pl.BlockSpec(memory_space=pltpu.HBM)] * 4,
-            out_specs=(pl.BlockSpec(memory_space=pltpu.VMEM),) * 6,
+            in_specs=[pl.BlockSpec(memory_space=pltpu.HBM)] * 5,
+            out_specs=(pl.BlockSpec(memory_space=pltpu.VMEM),) * 5,
             scratch_shapes=[
                 pltpu.VMEM((ROWS, COLS, SPAN), f32),
                 pltpu.VMEM((2, ROWS, 8, SPAN), f32),
                 pltpu.VMEM((2, ROWS, COLS), jnp.int32),
                 pltpu.VMEM((2, ROWS, SPAN), jnp.int32),
                 pltpu.VMEM((3, SPAN, SPAN), jnp.bfloat16),
+                pltpu.VMEM((2, 2, SPAN, SPAN), jnp.bfloat16),
+                pltpu.VMEM((2, LANES, LANES), f32),
                 pltpu.VMEM((BROWS, 3 * HALVES[0], SPAN), jnp.bfloat16),
                 pltpu.VMEM((BROWS, 3 * HALVES[1], SPAN), jnp.bfloat16),
                 pltpu.VMEM((BROWS + 2, HELD, OUT), f32),
+                pltpu.VMEM((2, BROWS, 8, LANES), f32),
                 pltpu.VMEM((2, 2 * BROWS, OUT), f32),
+                pltpu.VMEM((2, 2, 2 * BROWS, LANES), f32),
                 pltpu.VMEM((2, BROWS, 8, LANES), f32),
                 pltpu.VMEM((2, 8, LANES), f32),
                 pltpu.VMEM((HELD, OUT), f32),
@@ -472,7 +495,7 @@
             ),
             name="finish",
             out_shape=jax.ShapeDtypeStruct((BROWS, BCOLS, OUT), f32),
-            in_specs=[pl.BlockSpec(memory_space=pltpu.VMEM)] * 6,
+            in_specs=[pl.BlockSpec(memory_space=pltpu.VMEM)] * 5,
             out_specs=pl.BlockSpec(memory_space=pltpu.HBM),
             scratch_shapes=[
                 pltpu.VMEM((2, BROWS, BCOLS, LANES), f32),

time: 10.6 us -> 10.5 us (level)
    pallas_call x1, Pallas kernels: 1.28 us -> 1.04 us  [shards(): pl.pallas_call(lambda *refs: pl.run_scoped(lambda sems: finish(sems, *ref...]
    pallas_call x1, Pallas kernels: 9.14 us -> 9.35 us  [shards(): pl.pallas_call(functools.partial(scoped, n_xl, n_ta), name='stack_resampl...]
where the time goes in v8:
time: 10.5 us; the launch traced here: 10.4 us
  Pallas kernels  10.4 us (99%)
    pallas_call x1, Pallas kernels, shards(): pl.pallas_call(functools.partial(scoped, n_xl, n_ta), name='stack_resampl...  9.35 us
    pallas_call x1, Pallas kernels, shards(): pl.pallas_call(lambda *refs: pl.run_scoped(lambda sems: finish(sems, *ref...  1.04 us

profile of v8, /device:TPU:227, one launch (start us, length us, event | category | flops | bytes accessed | tf_op | source)
XLA Modules:
  0.0 10.4 jit_solution(2500876423132062180)
XLA Ops:
  0.0 9.3 %stack_resample.1 = (f32[8,104,384]{2,1,0:T(8,128)S(1)}, f32[2,8,128]{2,1,0:T(8,128)S(1)}, f32[2,64,256]{2,1,0:T(8,128)S(1)}, f32[2,2,8,128]{3,2,1,0:T(8,128)S(1)}, f32[2,2,1,128]{3,2,1,0:T(1,128)S(1)}) custom-call(f32[16,208,256]{2,1,0:T(8,128)} %refs_0_.1, s32[2,16,208]{2,1,0:T(8,128)} %refs_1_.1, bf16[3,256,256]{2,1,0:T(8,128)(2,1)} %constant.6.clone.refs_2_, ...), custom_call_target="tpu_custom_call" | custom-call | tf_op jit(solution)/shard_map/stack_resample/pallas_call | solution.py:453
  9.4 1.0 %finish.1 = f32[8,104,384]{2,1,0:T(8,128)} custom-call(f32[8,104,384]{2,1,0:T(8,128)S(1)} %get-tuple-element.10.refs_0_, f32[2,8,128]{2,1,0:T(8,128)S(1)} %get-tuple-element.11.refs_1_, f32[2,64,256]{2,1,0:T(8,128)S(1)} %get-tuple-element.12.refs_2_, f32[2,2,8,128]{3,2,1,0:T(8,128)S(1)} %get-tuple-element.13.refs_3_, ...), custom_call_target="tpu_custom_call" | custom-call | tf_op jit(solution)/shard_map/finish/pallas_call | solution.py:492

commit v9 on v8

--- a/solution.py
+++ b/solution.py
@@ -118,7 +118,7 @@
             condition = both(there(sign * dx, xl, n_xl), there(sign * dt, ta, n_ta))
 
             def run(dx=dx, dt=dt):
-                for di in (0, 1):
+                for di in (1, 0):
                     if (di, dx, dt) != (0, 0, 0):
                         action((di, dx, dt))
 

time: 10.5 us -> 10.3 us (0.981); the launches traced: 10.4 us -> 10.1 us
  Pallas kernels: 10.4 us -> 10.1 us
    pallas_call x1, Pallas kernels: 9.35 us -> 9.04 us  [shards(): pl.pallas_call(functools.partial(scoped, n_xl, n_ta), name='stack_resampl...]
where the time goes in v9:
time: 10.3 us; the launch traced here: 10.1 us
  Pallas kernels  10.1 us (98%)
    pallas_call x1, Pallas kernels, shards(): pl.pallas_call(functools.partial(scoped, n_xl, n_ta), name='stack_resampl...  9.04 us
    pallas_call x1, Pallas kernels, shards(): pl.pallas_call(lambda *refs: pl.run_scoped(lambda sems: finish(sems, *ref...  1.04 us

profile of v9, /device:TPU:227, one launch (start us, length us, event | category | flops | bytes accessed | tf_op | source)
XLA Modules:
  0.0 10.1 jit_solution(10504837629183446925)
XLA Ops:
  0.0 9.0 %stack_resample.1 = (f32[8,104,384]{2,1,0:T(8,128)S(1)}, f32[2,8,128]{2,1,0:T(8,128)S(1)}, f32[2,64,256]{2,1,0:T(8,128)S(1)}, f32[2,2,8,128]{3,2,1,0:T(8,128)S(1)}, f32[2,2,1,128]{3,2,1,0:T(1,128)S(1)}) custom-call(f32[16,208,256]{2,1,0:T(8,128)} %refs_0_.1, s32[2,16,208]{2,1,0:T(8,128)} %refs_1_.1, bf16[3,256,256]{2,1,0:T(8,128)(2,1)} %constant.6.clone.refs_2_, ...), custom_call_target="tpu_custom_call" | custom-call | tf_op jit(solution)/shard_map/stack_resample/pallas_call | solution.py:453
  9.1 1.0 %finish.1 = f32[8,104,384]{2,1,0:T(8,128)} custom-call(f32[8,104,384]{2,1,0:T(8,128)S(1)} %get-tuple-element.10.refs_0_, f32[2,8,128]{2,1,0:T(8,128)S(1)} %get-tuple-element.11.refs_1_, f32[2,64,256]{2,1,0:T(8,128)S(1)} %get-tuple-element.12.refs_2_, f32[2,2,8,128]{3,2,1,0:T(8,128)S(1)} %get-tuple-element.13.refs_3_, ...), custom_call_target="tpu_custom_call" | custom-call | tf_op jit(solution)/shard_map/finish/pallas_call | solution.py:492
